TPU v7x, 32 devices: a whole 2x2x4 slice. The times are simulated.
32 devices in a mesh: dp: 2 (over x), model: 4 (over z), ctx: 4 (over y, core).
Axes of the slice: x: 2, y: 2, z: 4, core: 2. Of those that a mesh axis runs over, the one named last changes fastest.
Arguments:
- x_tokens: bfloat16 [4096, 2560], P(('dp', 'ctx')), parts along dimension 0
- positions: int32 [4096], P(('dp', 'ctx')), parts along dimension 0
- w_dq: bfloat16 [2560, 768], replicated
- gain_q: float32 [768], replicated
- w_uq: bfloat16 [768, 2560], P(None, 'model')
- w_qr: bfloat16 [768, 1280], P(None, 'model')
- w_dkv: bfloat16 [2560, 256], replicated
- gain_kv: float32 [256], replicated
- w_kr: bfloat16 [2560, 32], replicated
- w_uk: bfloat16 [256, 2560], P(None, 'model')
- w_uv: bfloat16 [256, 2560], P(None, 'model')
- w_out: bfloat16 [2560, 2560], P('model')
Outputs:
- output: bfloat16 [4096, 2560], P(('dp', 'ctx', 'model')), parts along dimension 0
There are 2 independent parts. A program takes and returns all parts, laid end to end along the dimension named above; an argument that names none is the same for every part.
All inputs are finite; a program needn't handle non-finite values.
Results may differ from a plain program's by a relative error of at most 0.0080343.
Values are sent between devices in bfloat16 or wider.
A program may use at most 1 GiB of HBM per device.

v0:
```python
import jax
import jax.numpy as jnp
from jax import lax
from jax.sharding import PartitionSpec as P

NORM_EPS = 1e-6
ROPE_BASE = 10000.0
NEG_BIG = -1e30


def rms_norm(hidden, gain):
    mean_sq = jnp.mean(hidden * hidden, axis=-1, keepdims=True)
    return (hidden * lax.rsqrt(mean_sq + NORM_EPS) * gain).astype(jnp.bfloat16)


def apply_rope(vals, positions):
    half_dim = vals.shape[-1] // 2
    inv_freq = ROPE_BASE ** (-(jnp.arange(half_dim, dtype=jnp.float32) * 2.0 / vals.shape[-1]))
    angles = positions.astype(jnp.float32)[:, None] * inv_freq[None, :]
    angles = angles.reshape((vals.shape[0],) + (1,) * (vals.ndim - 2) + (half_dim,))
    cos_ang = jnp.cos(angles)
    sin_ang = jnp.sin(angles)
    lower_half = vals[..., :half_dim]
    upper_half = vals[..., half_dim:]
    return jnp.concatenate([lower_half * cos_ang - upper_half * sin_ang, upper_half * cos_ang + lower_half * sin_ang], axis=-1)


def project(x_tokens, positions, w_dq, gain_q, w_uq, w_qr, w_dkv, gain_kv, w_kr):
    tok_rows = x_tokens.shape[0]
    rope_dim = w_kr.shape[1]
    heads_loc = w_qr.shape[1] // rope_dim
    c_q = rms_norm(jnp.dot(x_tokens, w_dq, preferred_element_type=jnp.float32), gain_q)
    q_nope = jnp.dot(c_q, w_uq, preferred_element_type=jnp.float32).astype(jnp.bfloat16).reshape(tok_rows, heads_loc, -1)
    q_rope = apply_rope(jnp.dot(c_q, w_qr, preferred_element_type=jnp.float32).reshape(tok_rows, heads_loc, rope_dim), positions).astype(jnp.bfloat16)
    c_kv = rms_norm(jnp.dot(x_tokens, w_dkv, preferred_element_type=jnp.float32), gain_kv)
    k_rope = apply_rope(jnp.dot(x_tokens, w_kr, preferred_element_type=jnp.float32), positions).astype(jnp.bfloat16)
    return q_nope, q_rope, jnp.concatenate([c_kv, k_rope], axis=-1)


def up_project(latent_blk, w_uk, w_uv, heads_loc):
    kv_rank = w_uk.shape[0]
    tok_rows = latent_blk.shape[0]
    c_blk = latent_blk[:, :kv_rank]
    keys_blk = jnp.dot(c_blk, w_uk, preferred_element_type=jnp.float32).astype(jnp.bfloat16).reshape(tok_rows, heads_loc, -1)
    vals_blk = jnp.dot(c_blk, w_uv, preferred_element_type=jnp.float32).astype(jnp.bfloat16).reshape(tok_rows, heads_loc, -1)
    return keys_blk, vals_blk, latent_blk[:, kv_rank:]


def merge_block(run_state, q_nope, q_rope, q_pos, keys_blk, vals_blk, kr_blk, k_pos):
    m_run, l_run, acc_run = run_state
    score_scale = (q_nope.shape[-1] + q_rope.shape[-1]) ** -0.5
    scores = (jnp.einsum('qhd,khd->qhk', q_nope, keys_blk, preferred_element_type=jnp.float32) + jnp.einsum('qhr,kr->qhk', q_rope, kr_blk, preferred_element_type=jnp.float32)) * score_scale
    allowed = (k_pos[None, :] <= q_pos[:, None])[:, None, :]
    scores = jnp.where(allowed, scores, NEG_BIG)
    m_new = jnp.maximum(m_run, jnp.max(scores, axis=-1))
    exp_scores = jnp.where(allowed, jnp.exp(scores - m_new[..., None]), 0.0)
    rescale = jnp.exp(m_run - m_new)
    l_new = rescale * l_run + jnp.sum(exp_scores, axis=-1)
    acc_new = rescale[..., None] * acc_run + jnp.einsum('qhk,khd->qhd', exp_scores.astype(jnp.bfloat16), vals_blk, preferred_element_type=jnp.float32)
    return m_new, l_new, acc_new


def solution(mesh):
    ctx_size = mesh.shape['ctx']
    shift_perm = [(src_dev, (src_dev + 1) % ctx_size) for src_dev in range(ctx_size)]

    def local(x_tokens, positions, w_dq, gain_q, w_uq, w_qr, w_dkv, gain_kv, w_kr, w_uk, w_uv, w_out):
        q_nope, q_rope, latent = project(x_tokens, positions, w_dq, gain_q, w_uq, w_qr, w_dkv, gain_kv, w_kr)
        tok_rows = q_nope.shape[0]
        heads_loc = q_nope.shape[1]
        v_dim = w_uv.shape[1] // heads_loc
        start_state = (jnp.full((tok_rows, heads_loc), NEG_BIG, jnp.float32), jnp.zeros((tok_rows, heads_loc), jnp.float32), jnp.zeros((tok_rows, heads_loc, v_dim), jnp.float32))
        keys_blk, vals_blk, kr_blk = up_project(latent, w_uk, w_uv, heads_loc)
        first_state = merge_block(start_state, q_nope, q_rope, positions, keys_blk, vals_blk, kr_blk, positions)

        def hop(hop_idx, carry):
            run_state, latent_blk, pos_blk = carry
            latent_blk = lax.ppermute(latent_blk, 'ctx', shift_perm)
            pos_blk = lax.ppermute(pos_blk, 'ctx', shift_perm)
            keys_in, vals_in, kr_in = up_project(latent_blk, w_uk, w_uv, heads_loc)
            run_state = merge_block(run_state, q_nope, q_rope, positions, keys_in, vals_in, kr_in, pos_blk)
            return run_state, latent_blk, pos_blk

        final_state = lax.fori_loop(1, ctx_size, hop, (first_state, latent, positions))[0]
        out_heads = (final_state[2] / final_state[1][..., None]).astype(jnp.bfloat16).reshape(tok_rows, heads_loc * v_dim)
        y_part = jnp.dot(out_heads, w_out, preferred_element_type=jnp.float32)
        return lax.psum_scatter(y_part, 'model', scatter_dimension=0, tiled=True).astype(jnp.bfloat16)

    in_specs = (P(('dp', 'ctx'), None), P(('dp', 'ctx')), P(), P(), P(None, 'model'), P(None, 'model'), P(), P(), P(), P(None, 'model'), P(None, 'model'), P('model', None))
    out_specs = P(('dp', 'ctx', 'model'), None)
    return jax.shard_map(local, mesh=mesh, in_specs=in_specs, out_specs=out_specs, check_vma=False)
```

profile of v0, /device:TPU:0, one launch (start us, length us, event | category | flops | bytes accessed | tf_op | source)
XLA Modules:
  0.0 244.2 jit_solution(8226262563100311455)
XLA Ops:
  9.2 3.4 %fusion.43 = f32[512,32]{0,1:T(8,128)} fusion(bf16[512,2560]{1,0:T(8,128)(2,1)} %param.14, bf16[2560,32]{0,1:T(8,128)(2,1)} %param.22), kind=kOutput, calls=%fused_computation.66 | convolution fusion | flops 83886080 | bytes 2850816 | tf_op jit(solution)/shard_map/dot_general | solution.py:36
  22.3 5.3 %multiply_reduce_fusion = (f32[512]{0:T(512)S(1)}, f32[512,768]{1,0:T(8,128)S(1)}) fusion(bf16[512,2560]{1,0:T(8,128)(2,1)} %param.14, bf16[2560,768]{1,0:T(8,128)(2,1)} %param.16), kind=kOutput, calls=%fused_computation.32 | convolution fusion | flops 2014051840 | bytes 8128512 | tf_op jit(solution)/shard_map/dot_general | solution.py:32
  37.5 2.8 %fusion.42 = f32[10,512,512]{2,1,0:T(8,128)S(1)} fusion(bf16[512,10,64]{0,2,1:T(8,128)(2,1)} %bitcast.85, bf16[512,10,64]{0,2,1:T(8,128)(2,1)} %bitcast.82), kind=kOutput, calls=%fused_computation.65 | convolution fusion | flops 335544320 | bytes 11796480 | tf_op jit(solution)/shard_map/qhd,khd->qhk/dot_general | solution.py:52
  40.3 2.5 %fusion.40 = (f32[512,10]{0,1:T(8,128)S(1)}, f32[512,10,512]{0,2,1:T(8,128)S(1)}) fusion(bf16[512,16]{0,1:T(8,128)(2,1)S(1)} %get-tuple-element.110, bf16[512,16]{0,1:T(8,128)(2,1)S(1)} %get-tuple-element.111, bf16[512,10,16]{0,2,1:T(8,128)(2,1)S(1)} %get-tuple-element.103, bf16[512,10,16]{0,2,1:T(8,128)(2,1)S(1)} %get-tuple-element.102, ...), kind=kOutput, calls=%fused_computation.63 | convolution fusion | flops 178973696 | bytes 21614592 | tf_op jit(solution)/shard_map/qhr,kr->qhk/dot_general | solution.py:52
  45.3 3.2 %fusion.30 = f32[512,10,64]{0,2,1:T(8,128)} fusion(bf16[512,10,64]{0,2,1:T(8,128)(2,1)S(1)} %bitcast.84, f32[512,10,512]{0,2,1:T(8,128)S(1)} %get-tuple-element.117, f32[512,10]{0,1:T(8,128)S(1)} %broadcast_maximum_fusion, pred[512,512]{0,1:T(8,128)(4,1)S(1)} %broadcast_compare_fusion.1, f32[512,10]{0,1:T(8,128)S(1)} %get-tuple-element.106), kind=kOutput, calls=%fused_computation.34 | convolution fusion | flops 343736320 | bytes 12754944 | tf_op jit(solution)/shard_map/qhk,khd->qhd/dot_general | solution.py:59
  48.5 84.9 %while.18 = (s32[]{:T(128)}, f32[512,10]{0,1:T(8,128)}, f32[512,10]{0,1:T(8,128)}, f32[512,10,64]{0,2,1:T(8,128)}, bf16[512,288]{0,1:T(8,128)(2,1)}, /*index=5*/...) while((s32[]{:T(128)}, f32[512,10]{0,1:T(8,128)}, ...), condition=%wide.region_7.8_spmd, body=%wide.region_4.7_spmd.sunk | while | flops 1202202624 | bytes 80314752 | solution.py:84
  49.0 2.6 %collective-permute-start.1 = (s32[512]{0:T(512)S(1)}, s32[512]{0:T(512)S(1)}, u32[]{:S(2)}, u32[]{:S(2)}) collective-permute-start(s32[512]{0:T(512)S(1)} %get-tuple-element.210), channel_id=1, source_target_pairs={{0,1},{1,2},{2,3},{3,0},{4,5},{5,6},{6,7},{7,4},{8,9},{9,10},{10,1... | collective-permute-start | bytes 6152 | tf_op jit(solution)/shard_map/while/body/eval_jaxpr/ppermute | solution.py:79
  51.6 3.8 %collective-permute-done.1 = s32[512]{0:T(512)S(1)} collective-permute-done((s32[512]{0:T(512)S(1)}, s32[512]{0:T(512)S(1)}, u32[]{:S(2)}, u32[]{:S(2)}) %collective-permute-start.1) | collective-permute-done | bytes 2080 | tf_op jit(solution)/shard_map/while/body/eval_jaxpr/ppermute | solution.py:79
  55.6 2.3 convolution_convert_fusion.8
  60.1 2.3 convolution_convert_fusion.7
  64.5 2.9 %fusion.90 = f32[10,512,512]{2,1,0:T(8,128)S(1)} fusion(bf16[512,10,64]{0,2,1:T(8,128)(2,1)} %bitcast.81, bf16[512,10,64]{0,2,1:T(8,128)(2,1)} %get-tuple-element.225), kind=kOutput, calls=%fused_computation.64.clone.1 | convolution fusion | flops 335544320 | bytes 11796480 | tf_op jit(solution)/shard_map/while/body/eval_jaxpr/qhd,khd->qhk/dot_general | solution.py:52
  67.5 3.2 %fusion.91 = (f32[512,10]{0,1:T(8,128)S(1)}, f32[512,10,512]{0,2,1:T(8,128)S(1)}) fusion(bf16[512,10,32]{0,2,1:T(8,128)(2,1)S(1)} %copy-done.5, bf16[512,288]{0,1:T(8,128)(2,1)} %collective-permute-done, f32[10,512,512]{2,1,0:T(8,128)S(1)} %fusion.90, pred[512,512]{0,1:T(8,128)(4,1)S(1)} %broadcast_compare_fusion.3), kind=kOutput, calls=%fused_computation.62.clone.1 | convolution fusion | flops 178252800 | bytes 21614592 | tf_op jit(solution)/shard_map/while/body/eval_jaxpr/qhr,kr->qhk/dot_general | solution.py:52
  77.2 2.4 collective-permute-start.1
  79.7 3.8 %collective-permute-done.1 = s32[512]{0:T(512)S(1)} collective-permute-done((s32[512]{0:T(512)S(1)}, s32[512]{0:T(512)S(1)}, u32[]{:S(2)}, u32[]{:S(2)}) %collective-permute-start.1) | collective-permute-done | bytes 2080 | tf_op jit(solution)/shard_map/while/body/eval_jaxpr/ppermute | solution.py:79
  83.6 2.3 convolution_convert_fusion.8
  92.6 2.9 %fusion.90 = f32[10,512,512]{2,1,0:T(8,128)S(1)} fusion(bf16[512,10,64]{0,2,1:T(8,128)(2,1)} %bitcast.81, bf16[512,10,64]{0,2,1:T(8,128)(2,1)} %get-tuple-element.225), kind=kOutput, calls=%fused_computation.64.clone.1 | convolution fusion | flops 335544320 | bytes 11796480 | tf_op jit(solution)/shard_map/while/body/eval_jaxpr/qhd,khd->qhk/dot_general | solution.py:52
  95.5 3.2 %fusion.91 = (f32[512,10]{0,1:T(8,128)S(1)}, f32[512,10,512]{0,2,1:T(8,128)S(1)}) fusion(bf16[512,10,32]{0,2,1:T(8,128)(2,1)S(1)} %copy-done.5, bf16[512,288]{0,1:T(8,128)(2,1)} %collective-permute-done, f32[10,512,512]{2,1,0:T(8,128)S(1)} %fusion.90, pred[512,512]{0,1:T(8,128)(4,1)S(1)} %broadcast_compare_fusion.3), kind=kOutput, calls=%fused_computation.62.clone.1 | convolution fusion | flops 178252800 | bytes 21614592 | tf_op jit(solution)/shard_map/while/body/eval_jaxpr/qhr,kr->qhk/dot_general | solution.py:52
  105.3 2.4 collective-permute-start.1
  107.7 3.8 %collective-permute-done.1 = s32[512]{0:T(512)S(1)} collective-permute-done((s32[512]{0:T(512)S(1)}, s32[512]{0:T(512)S(1)}, u32[]{:S(2)}, u32[]{:S(2)}) %collective-permute-start.1) | collective-permute-done | bytes 2080 | tf_op jit(solution)/shard_map/while/body/eval_jaxpr/ppermute | solution.py:79
  111.7 2.3 convolution_convert_fusion.8
  120.6 2.9 %fusion.90 = f32[10,512,512]{2,1,0:T(8,128)S(1)} fusion(bf16[512,10,64]{0,2,1:T(8,128)(2,1)} %bitcast.81, bf16[512,10,64]{0,2,1:T(8,128)(2,1)} %get-tuple-element.225), kind=kOutput, calls=%fused_computation.64.clone.1 | convolution fusion | flops 335544320 | bytes 11796480 | tf_op jit(solution)/shard_map/while/body/eval_jaxpr/qhd,khd->qhk/dot_general | solution.py:52
  123.6 3.2 %fusion.91 = (f32[512,10]{0,1:T(8,128)S(1)}, f32[512,10,512]{0,2,1:T(8,128)S(1)}) fusion(bf16[512,10,32]{0,2,1:T(8,128)(2,1)S(1)} %copy-done.5, bf16[512,288]{0,1:T(8,128)(2,1)} %collective-permute-done, f32[10,512,512]{2,1,0:T(8,128)S(1)} %fusion.90, pred[512,512]{0,1:T(8,128)(4,1)S(1)} %broadcast_compare_fusion.3), kind=kOutput, calls=%fused_computation.62.clone.1 | convolution fusion | flops 178252800 | bytes 21614592 | tf_op jit(solution)/shard_map/while/body/eval_jaxpr/qhr,kr->qhk/dot_general | solution.py:52
  134.8 4.5 %fusion.44 = f32[512,2560]{1,0:T(8,128)} fusion(bf16[512,640]{0,1:T(8,128)(2,1)S(1)} %bitcast.86, bf16[640,2560]{1,0:T(8,128)(2,1)S(1)} %copy-done), kind=kOutput, calls=%fused_computation.67 | convolution fusion | flops 1677721600 | bytes 9175040 | tf_op jit(solution)/shard_map/dot_general | solution.py:86
  139.4 95.7 %reduce-scatter.2.cloned.1.call-done = f32[128,2560]{1,0:T(8,128)} async-done(((f32[512,2560]{1,0:T(8,128)}), f32[128,2560]{1,0:T(8,128)}) %reduce-scatter.2.cloned.1.call-update) | async-done | bytes 1310736 | tf_op jit(solution)/shard_map/reduce_scatter | solution.py:87
  (130 shorter events, 66.5 us)
Async XLA Ops:
  6.5 128.3 %copy-start = (bf16[640,2560]{1,0:T(8,128)(2,1)S(1)}, bf16[640,2560]{1,0:T(8,128)(2,1)}, u32[]{:S(2)}) copy-start(bf16[640,2560]{1,0:T(8,128)(2,1)} %param.25) | copy-start | bytes 9830404
  6.5 228.6 %reduce-scatter.2.cloned.1.call-start = ((), (), s32[]{:S(2)}) async-start(), calls=%async_computation.1 | async-start | bytes 6553600 | tf_op jit(solution)/shard_map/reduce_scatter | solution.py:87
  9.2 3.4 %copy-start.6 = (bf16[512,2560]{1,0:T(8,128)(2,1)S(1)}, bf16[512,2560]{1,0:T(8,128)(2,1)}, u32[]{:S(2)}) copy-start(bf16[512,2560]{1,0:T(8,128)(2,1)} %param.14) | copy-start | bytes 7864324
  9.2 3.4 %copy-start.18 = (bf16[2560,256]{1,0:T(8,128)(2,1)S(1)}, bf16[2560,256]{1,0:T(8,128)(2,1)}, u32[]{:S(2)}) copy-start(bf16[2560,256]{1,0:T(8,128)(2,1)} %param.20) | copy-start | bytes 3932164
  22.3 5.3 %copy-start.14 = (bf16[768,320]{0,1:T(8,128)(2,1)S(1)}, bf16[768,320]{0,1:T(8,128)(2,1)}, u32[]{:S(2)}) copy-start(bf16[768,320]{0,1:T(8,128)(2,1)} %param.19) | copy-start | bytes 1474564
  22.3 5.3 %copy-start.16 = (f32[768]{0:T(1024)S(1)}, f32[768]{0:T(1024)}, u32[]{:S(2)}) copy-start(f32[768]{0:T(1024)} %param.17) | copy-start | bytes 9220
  22.3 6.7 %copy-start.13 = (bf16[768,640]{1,0:T(8,128)(2,1)S(1)}, bf16[768,640]{1,0:T(8,128)(2,1)}, u32[]{:S(2)}) copy-start(bf16[768,640]{1,0:T(8,128)(2,1)} %param.18) | copy-start | bytes 2949124
  45.3 3.2 %copy-start.15 = (s32[512]{0:T(512)S(1)}, s32[512]{0:T(512)}, u32[]{:S(2)}) copy-start(s32[512]{0:T(512)} %param.15) | copy-start | bytes 6148
  48.5 7.1 %collective-permute-start = (bf16[512,288]{0,1:T(8,128)(2,1)}, bf16[512,288]{0,1:T(8,128)(2,1)}, u32[]{:S(2)}, u32[]{:S(2)}) collective-permute-start(bf16[512,288]{0,1:T(8,128)(2,1)} %get-tuple-element.209), channel_id=1, source_target_pairs={{0,1},{1,2},{2,3},{3,0},{4,5},{5,6},{6,7},{7,4},{8,9},{9,10},{10,1... | collective-permute-start | bytes 884744 | tf_op jit(solution)/shard_map/while/body/eval_jaxpr/ppermute | solution.py:78
  49.0 6.4 %collective-permute-start.1 = (s32[512]{0:T(512)S(1)}, s32[512]{0:T(512)S(1)}, u32[]{:S(2)}, u32[]{:S(2)}) collective-permute-start(s32[512]{0:T(512)S(1)} %get-tuple-element.210), channel_id=1, source_target_pairs={{0,1},{1,2},{2,3},{3,0},{4,5},{5,6},{6,7},{7,4},{8,9},{9,10},{10,1... | collective-permute-start | bytes 6152 | tf_op jit(solution)/shard_map/while/body/eval_jaxpr/ppermute | solution.py:79
  64.5 2.9 %copy-start.5 = (bf16[512,10,32]{0,2,1:T(8,128)(2,1)S(1)}, bf16[512,10,32]{0,2,1:T(8,128)(2,1)}, u32[]{:S(2)}) copy-start(bf16[512,10,32]{0,2,1:T(8,128)(2,1)} %get-tuple-element.226) | copy-start | bytes 983044 | tf_op jit(solution)/shard_map/while
  67.5 3.2 %copy-start.8 = (f32[512,10]{0,1:T(8,128)S(1)}, f32[512,10]{0,1:T(8,128)}, u32[]{:S(2)}) copy-start(f32[512,10]{0,1:T(8,128)} %get-tuple-element.206) | copy-start | bytes 61444 | tf_op jit(solution)/shard_map/while
  70.7 2.5 %copy-start.1 = (bf16[512,640]{0,1:T(8,128)(2,1)S(1)}, bf16[512,640]{0,1:T(8,128)(2,1)}, u32[]{:S(2)}) copy-start(bf16[512,640]{0,1:T(8,128)(2,1)} %copy.33) | copy-start | bytes 1966084 | tf_op jit(solution)/shard_map/while
  72.6 2.7 %copy-start.12 = (f32[512,10]{0,1:T(8,128)}, f32[512,10]{0,1:T(8,128)S(1)}, u32[]{:S(2)}) copy-start(f32[512,10]{0,1:T(8,128)S(1)} %get-tuple-element.219) | copy-start | bytes 61444 | tf_op jit(solution)/shard_map/while
  77.2 6.4 %collective-permute-start = (bf16[512,288]{0,1:T(8,128)(2,1)}, bf16[512,288]{0,1:T(8,128)(2,1)}, u32[]{:S(2)}, u32[]{:S(2)}) collective-permute-start(bf16[512,288]{0,1:T(8,128)(2,1)} %get-tuple-element.209), channel_id=1, source_target_pairs={{0,1},{1,2},{2,3},{3,0},{4,5},{5,6},{6,7},{7,4},{8,9},{9,10},{10,1... | collective-permute-start | bytes 884744 | tf_op jit(solution)/shard_map/while/body/eval_jaxpr/ppermute | solution.py:78
  77.2 6.2 %collective-permute-start.1 = (s32[512]{0:T(512)S(1)}, s32[512]{0:T(512)S(1)}, u32[]{:S(2)}, u32[]{:S(2)}) collective-permute-start(s32[512]{0:T(512)S(1)} %get-tuple-element.210), channel_id=1, source_target_pairs={{0,1},{1,2},{2,3},{3,0},{4,5},{5,6},{6,7},{7,4},{8,9},{9,10},{10,1... | collective-permute-start | bytes 6152 | tf_op jit(solution)/shard_map/while/body/eval_jaxpr/ppermute | solution.py:79
  92.6 2.9 %copy-start.5 = (bf16[512,10,32]{0,2,1:T(8,128)(2,1)S(1)}, bf16[512,10,32]{0,2,1:T(8,128)(2,1)}, u32[]{:S(2)}) copy-start(bf16[512,10,32]{0,2,1:T(8,128)(2,1)} %get-tuple-element.226) | copy-start | bytes 983044 | tf_op jit(solution)/shard_map/while
  95.5 3.2 %copy-start.8 = (f32[512,10]{0,1:T(8,128)S(1)}, f32[512,10]{0,1:T(8,128)}, u32[]{:S(2)}) copy-start(f32[512,10]{0,1:T(8,128)} %get-tuple-element.206) | copy-start | bytes 61444 | tf_op jit(solution)/shard_map/while
  100.7 2.7 %copy-start.12 = (f32[512,10]{0,1:T(8,128)}, f32[512,10]{0,1:T(8,128)S(1)}, u32[]{:S(2)}) copy-start(f32[512,10]{0,1:T(8,128)S(1)} %get-tuple-element.219) | copy-start | bytes 61444 | tf_op jit(solution)/shard_map/while
  105.3 6.4 %collective-permute-start = (bf16[512,288]{0,1:T(8,128)(2,1)}, bf16[512,288]{0,1:T(8,128)(2,1)}, u32[]{:S(2)}, u32[]{:S(2)}) collective-permute-start(bf16[512,288]{0,1:T(8,128)(2,1)} %get-tuple-element.209), channel_id=1, source_target_pairs={{0,1},{1,2},{2,3},{3,0},{4,5},{5,6},{6,7},{7,4},{8,9},{9,10},{10,1... | collective-permute-start | bytes 884744 | tf_op jit(solution)/shard_map/while/body/eval_jaxpr/ppermute | solution.py:78
  105.3 6.2 %collective-permute-start.1 = (s32[512]{0:T(512)S(1)}, s32[512]{0:T(512)S(1)}, u32[]{:S(2)}, u32[]{:S(2)}) collective-permute-start(s32[512]{0:T(512)S(1)} %get-tuple-element.210), channel_id=1, source_target_pairs={{0,1},{1,2},{2,3},{3,0},{4,5},{5,6},{6,7},{7,4},{8,9},{9,10},{10,1... | collective-permute-start | bytes 6152 | tf_op jit(solution)/shard_map/while/body/eval_jaxpr/ppermute | solution.py:79
  120.6 2.9 %copy-start.5 = (bf16[512,10,32]{0,2,1:T(8,128)(2,1)S(1)}, bf16[512,10,32]{0,2,1:T(8,128)(2,1)}, u32[]{:S(2)}) copy-start(bf16[512,10,32]{0,2,1:T(8,128)(2,1)} %get-tuple-element.226) | copy-start | bytes 983044 | tf_op jit(solution)/shard_map/while
  123.6 3.2 %copy-start.8 = (f32[512,10]{0,1:T(8,128)S(1)}, f32[512,10]{0,1:T(8,128)}, u32[]{:S(2)}) copy-start(f32[512,10]{0,1:T(8,128)} %get-tuple-element.206) | copy-start | bytes 61444 | tf_op jit(solution)/shard_map/while
  128.7 2.7 %copy-start.12 = (f32[512,10]{0,1:T(8,128)}, f32[512,10]{0,1:T(8,128)S(1)}, u32[]{:S(2)}) copy-start(f32[512,10]{0,1:T(8,128)S(1)} %get-tuple-element.219) | copy-start | bytes 61444 | tf_op jit(solution)/shard_map/while
  (16 other events, 32.2 us)
Sparse Core Ops, SparseCore 0:
  139.5 95.5 reduce-scatter.1
where the time goes:
time: 245 us; the launch traced here: 244 us
  waiting for transfers between devices  107 us (44%)
  matrix products  67.6 us (28%)
  local copies, waits for them, and re-layouts  28.8 us (12%)
  other arithmetic  18.8 us (8%)
  between operations  13.6 us (6%)
  starting transfers between devices  7.96 us (3%)
    reduce_scatter x1, waiting for transfers between devices, local(): lax.psum_scatter(y_part, 'model', scatter_dimension=0, tiled=True)  95.7 us
    dot_general x4, matrix products, merge_block(): jnp.einsum('qhr,kr->qhk', q_rope, kr_blk, preferred_element_type=jnp.floa...  12.2 us
    dot_general x4, matrix products, merge_block(): jnp.einsum('qhd,khd->qhk', q_nope, keys_blk, preferred_element_type=jnp.f...  11.5 us
    ppermute x3, waiting for transfers between devices, hop(): pos_blk = lax.ppermute(pos_blk, 'ctx', shift_perm)  11.3 us
    dot_general x4, matrix products, merge_block(): jnp.einsum('qhk,khd->qhd', exp_scores.astype(jnp.bfloat16), vals_blk, pre...  9.36 us
    dot_general x4, matrix products, up_project(): jnp.dot(c_blk, w_uk, preferred_element_type=jnp.float32)  9.17 us
    convert_element_type x4, local copies, waits for them, and re-layouts, up_project(): jnp.dot(c_blk, w_uv, preferred_element_type=jnp.float32)  8.73 us
    convert_element_type x4, local copies, waits for them, and re-layouts, up_project(): jnp.dot(c_blk, w_uk, preferred_element_type=jnp.float32)  8.7 us
  transfers between devices with their start and end apart: 7, of which 4 were waited for; matrix products, arithmetic and copies ran while one was open for 0% of the time, Pallas kernels for 0%

commit v1 on v0

v1 whole, which is shorter than its diff:
```python
import functools

import jax
import jax.numpy as jnp
import numpy as np
from jax import lax
from jax.experimental import pallas as pl
from jax.experimental.pallas import tpu as pltpu
from jax.sharding import PartitionSpec as P

MESH = pl.DeviceIdType.MESH
F32 = jnp.float32
BF16 = jnp.bfloat16

HIDDEN = 2560
Q_RANK = 768
KV_RANK = 256
HEADS = 10
PAIRS = HEADS // 2
NOPE = 64
ROPE = 32
VDIM = 64
ROWS = 512
SPAN = 256
NSPAN = 8
CTX = 4
MODEL = 4
HV = HEADS * VDIM
NHALF = HIDDEN // 2
QROWS = HV // 4
KRP = SPAN // 8
EPS = 1e-6
ROPE_BASE = 10000.0
SM_SCALE = float((NOPE + ROPE) ** -0.5 * np.log2(np.e))
NEG = -1e30


def dot(a, b):
    return jnp.dot(a, b, preferred_element_type=F32)


def dot_nt(a, b):
    return lax.dot_general(a, b, (((1,), (1,)), ((), ())), preferred_element_type=F32)


def rms(h, gain):
    ms = jnp.mean(h * h, axis=-1, keepdims=True)
    return (h * lax.rsqrt(ms + EPS) * gain).astype(BF16)


def kernel(x_h, pos_r, freq_r, gq_r, gkv_r, wdq_h, wuq_h, wqr_h, wdkv_h, wkr_h, wuk_h, wuv_h, wout_h, out_h,
           x_v, wdq_v, wuq_v, wqr_v, wdkv_v, wkr_v, wkr4_v, wuk_v, wuv_v,
           cos_v, sin_v, tile_v, lat_v, cq_v, qm_v, k_v, v_v, kr_v, s_v, mx_v, mb_v, l_v, acc_v,
           os_v, oall_v, wall_v, yst_v,
           lsem, kv_ssem, kv_rsem, wz_own, wz_ssem, wz_rsem, wy_ssem, wy_rsem, wd_ssem, wd_rsem,
           oz_ssem, oz_rsem, ox_ssem, ox_rsem, yb_ssem, yb_rsem, yl_sem):
    dp = lax.axis_index('dp')
    z = lax.axis_index('model')
    ctx = lax.axis_index('ctx')
    partner = ctx + 1 - 2 * lax.rem(ctx, 2)
    ynbr = lax.rem(ctx + 2, CTX)
    diag = lax.rem(partner + 2, CTX)
    xn = 1 - dp

    def dev(d=None, m=None, c=None):
        return (dp if d is None else d, z if m is None else m, ctx if c is None else c)

    def remote(src, dst, ss, rs, where):
        return pltpu.make_async_remote_copy(src_ref=src, dst_ref=dst, send_sem=ss, recv_sem=rs,
                                            device_id=where, device_id_type=MESH)

    def local(src, dst, idx):
        return pltpu.make_async_copy(src, dst, lsem.at[idx])

    loads = [
        local(wkr_h, wkr_v, 0),
        local(x_h.at[pl.ds(0, SPAN)], x_v.at[pl.ds(0, SPAN)], 1),
        local(wdkv_h, wdkv_v, 2),
        local(x_h.at[pl.ds(SPAN, SPAN)], x_v.at[pl.ds(SPAN, SPAN)], 3),
        local(wdq_h, wdq_v, 4),
        local(wuq_h, wuq_v, 5),
        local(wqr_h, wqr_v, 6),
        local(wuk_h, wuk_v, 7),
        local(wuv_h, wuv_v, 8),
        local(wout_h.at[:, pl.ds(pl.multiple_of(dp * NHALF, 128), NHALF)], wall_v.at[z], 9),
    ]
    for c in loads:
        c.start()

    barrier = pltpu.get_barrier_semaphore()
    peers = [dev(m=lax.rem(z + d, MODEL)) for d in (1, 2, 3)] + [dev(d=xn), dev(c=partner), dev(c=ynbr)]
    for p in peers:
        pl.semaphore_signal(barrier, inc=1, device_id=p, device_id_type=MESH)
    pl.semaphore_wait(barrier, len(peers))

    def wpiece(s, c):
        return wall_v.at[s, pl.ds(pl.multiple_of(c * QROWS, 16), QROWS)]

    wout_src = wout_h.at[pl.ds(pl.multiple_of(ctx * QROWS, 16), QROWS), pl.ds(pl.multiple_of(dp * NHALF, 128), NHALF)]

    def w_own(up):
        return remote(wout_src, wpiece(z, ctx), wz_own.at[up], wz_rsem.at[z], dev(m=z + 2 * up - 1))

    def w_fwd_z(s, to):
        return remote(wpiece(s, ctx), wpiece(s, ctx), wz_ssem.at[s], wz_rsem.at[s], dev(m=to))

    def w_fwd_y(s):
        return remote(wpiece(s, ctx), wpiece(s, ctx), wy_ssem.at[s], wy_rsem.at[s], dev(c=ynbr))

    def w_fwd_d(s, which):
        c = ctx if which == 0 else ynbr
        return remote(wpiece(s, c), wpiece(s, c), wd_ssem.at[s, which], wd_rsem.at[s, which], dev(c=partner))

    def wait_wz(s):
        remote(wpiece(s, ctx), wpiece(s, ctx), wz_ssem.at[s], wz_rsem.at[s], dev()).wait_recv()

    def wait_wy(s):
        remote(wpiece(s, ynbr), wpiece(s, ynbr), wy_ssem.at[s], wy_rsem.at[s], dev()).wait_recv()

    def wait_wd(s, which):
        c = partner if which == 0 else diag
        remote(wpiece(s, c), wpiece(s, c), wd_ssem.at[s, which], wd_rsem.at[s, which], dev()).wait_recv()

    @pl.when(z < MODEL - 1)
    def _():
        w_own(1).start()

    @pl.when(z > 0)
    def _():
        w_own(0).start()

    def each_share(j, fn):
        for sign in (-1, 1):
            s = z + sign * j

            @pl.when((s >= 0) & (s < MODEL))
            def _(s=s, sign=sign):
                fn(s, sign)

    def w_hop(j):
        def step(s, sign):
            wait_wz(s)
            to = z - sign

            @pl.when((to >= 0) & (to < MODEL))
            def _():
                w_fwd_z(s, to).start()
            w_fwd_y(s).start()
            w_fwd_d(s, 0).start()
        each_share(j, step)

    def w_across(j):
        def step(s, sign):
            wait_wy(s)
            w_fwd_d(s, 1).start()
        each_share(j, step)

    lane = lax.broadcasted_iota(jnp.int32, (1, 128), 1)
    for g in range(ROWS // 128):
        row = pos_r[:, pl.ds(128 * g, 128)].astype(F32)
        col = jnp.transpose(jnp.broadcast_to(row, (128, 128)), (1, 0))
        ang = col * freq_r[...]
        cos_v[pl.ds(128 * g, 128), :] = jnp.cos(ang)
        sin_v[pl.ds(128 * g, 128), :] = jnp.sin(ang)
    rr = lax.broadcasted_iota(jnp.int32, (KV_RANK, 1024), 0)
    cc = lax.broadcasted_iota(jnp.int32, (KV_RANK, 1024), 1)
    tile_v[...] = jnp.where((rr // ROPE == cc // 128) & (rr % ROPE == cc % ROPE), 1.0, 0.0).astype(BF16)
    low = (lane % ROPE) < (ROPE // 2)

    def rope(v, r0):
        up = pltpu.roll(v, 128 - ROPE // 2, 1)
        dn = pltpu.roll(v, ROPE // 2, 1)
        rot = jnp.where(low, -up, dn)
        return v * cos_v[pl.ds(r0, SPAN), :] + rot * sin_v[pl.ds(r0, SPAN), :]

    loads[0].wait()
    t_r = lax.broadcasted_iota(jnp.int32, (ROPE, 128), 0)
    t_c = lax.broadcasted_iota(jnp.int32, (ROPE, 128), 1)
    rep = jnp.where(t_r == t_c % ROPE, 1.0, 0.0).astype(BF16)
    wkr4_v[...] = dot(wkr_v[...], rep).astype(BF16)
    for t in range(2):
        r0 = t * SPAN
        if t == 0:
            loads[1].wait()
            loads[2].wait()
        else:
            loads[3].wait()
        xs = x_v[pl.ds(r0, SPAN), :]
        lat_v[ctx, t, pl.ds(0, SPAN), :] = rms(dot(xs, wdkv_v[...]), gkv_r[...])
        kr = rope(dot(xs, wkr4_v[...]), r0)
        for half in range(2):
            packed = kr[128 * half:128 * half + KRP]
            for g in range(1, 4):
                a = 128 * half + KRP * g
                packed = jnp.where(lane // ROPE == g, kr[a:a + KRP], packed)
            lat_v[ctx, t, pl.ds(SPAN, KRP), pl.ds(128 * half, 128)] = packed.astype(BF16)

    def kv_copy(c, idx, to):
        return remote(lat_v.at[c], lat_v.at[c], kv_ssem.at[idx], kv_rsem.at[idx], dev(c=to))

    kv_copy(ctx, 0, ynbr).start()
    kv_copy(ctx, 1, partner).start()

    loads[4].wait()
    for t in range(2):
        cq_v[pl.ds(t * SPAN, SPAN), :] = rms(dot(x_v[pl.ds(t * SPAN, SPAN), :], wdq_v[...]), gq_r[...])
    loads[5].wait()
    loads[6].wait()
    for t in range(2):
        cq = cq_v[pl.ds(t * SPAN, SPAN), :]
        qn = dot(cq, wuq_v[...]).astype(BF16)
        zero = jnp.zeros((SPAN, 128), BF16)
        for p in range(PAIRS):
            blk = qn[:, 128 * p:128 * p + 128]
            qm_v[p, t, pl.ds(0, SPAN), pl.ds(0, 128)] = jnp.where(lane < NOPE, blk, zero)
            qm_v[p, t, pl.ds(SPAN, SPAN), pl.ds(0, 128)] = jnp.where(lane < NOPE, zero, blk)
        for b in range(3):
            w = wqr_v[:, pl.ds(128 * b, 128)] if b < 2 else jnp.concatenate([wqr_v[:, pl.ds(256, 64)]] * 2, axis=1)
            qr = rope(dot(cq, w), t * SPAN).astype(BF16)
            for h in range(4 * b, min(4 * b + 4, HEADS)):
                qm_v[h // 2, t, pl.ds(SPAN * (h % 2), SPAN), pl.ds(128, 128)] = jnp.where(lane // ROPE == h % 4, qr, zero)

    def up(c):
        for t in range(2):
            sp = c if t == 0 else NSPAN - 1 - c
            lat = lat_v[c, t, pl.ds(0, SPAN), :]
            k_v[sp] = dot(lat, wuk_v[...]).astype(BF16)
            v_v[sp] = dot(lat, wuv_v[...]).astype(BF16)
            big = dot(lat_v[c, t, pl.ds(SPAN, KRP), :], tile_v[...]).astype(BF16)
            for g in range(8):
                kr_v[sp, pl.ds(KRP * g, KRP), :] = big[:, 128 * g:128 * g + 128]

    loads[7].wait()
    loads[8].wait()
    up(ctx)
    kv_copy(partner, 1, ctx).wait_recv()
    up(partner)
    kv_copy(ynbr, 0, ctx).wait_recv()
    kv_copy(ynbr, 2, partner).start()
    up(ynbr)
    w_hop(1)
    kv_copy(diag, 2, ctx).wait_recv()
    up(diag)

    def block(b):
        if b < 5:
            return 1, NSPAN - 1 - ctx - b
        if b == 8:
            return 0, ctx
        hi = b < NSPAN - ctx
        return jnp.where(hi, 1, 0), jnp.where(hi, NSPAN - 1 - ctx - b, b - (NSPAN - ctx))

    ORDER = (0, 8, 1, 2, 3, 4, 5, 6, 7)
    q_i = lax.broadcasted_iota(jnp.int32, (SPAN, SPAN), 0)
    k_i = lax.broadcasted_iota(jnp.int32, (SPAN, SPAN), 1)
    causal = k_i <= q_i

    def scores(p, b):
        buf = p % 2
        qs, ks = block(b)
        kc = jnp.concatenate([k_v[ks, :, pl.ds(128 * p, 128)], kr_v[ks]], axis=1)
        for a in range(2):
            rows = pl.ds(SPAN * a, SPAN)
            s = dot_nt(qm_v[p, qs, rows, :], kc)
            if b in (0, 8):
                s = jnp.where(causal, s, NEG)
            s_v[buf, b, rows, :] = s
            m = jnp.maximum(s[:, :128], s[:, 128:])
            if b not in (0, 8):
                m = jnp.maximum(mx_v[buf, qs, rows, :], m)
            mx_v[buf, qs, rows, :] = m

    def maxima(p):
        buf = p % 2
        for qs in range(2):
            for a in range(2):
                rows = pl.ds(SPAN * a, SPAN)
                m = jnp.max(mx_v[buf, qs, rows, :], axis=1, keepdims=True)
                mb_v[qs, rows, :] = jnp.broadcast_to(m * SM_SCALE, (SPAN, 128))

    def values(p, b):
        buf = p % 2
        qs, ks = block(b)
        vb = v_v[ks, :, pl.ds(128 * p, 128)]
        for a in range(2):
            rows = pl.ds(SPAN * a, SPAN)
            m = mb_v[qs, rows, :]
            e0 = jnp.exp2(s_v[buf, b, rows, pl.ds(0, 128)] * SM_SCALE - m)
            e1 = jnp.exp2(s_v[buf, b, rows, pl.ds(128, 128)] * SM_SCALE - m)
            pv = dot(jnp.concatenate([e0.astype(BF16), e1.astype(BF16)], axis=1), vb)
            l = e0 + e1
            if b in (0, 8):
                l_v[qs, rows, :] = l
                acc_v[qs, rows, :] = pv
            else:
                l_v[qs, rows, :] += l
                acc_v[qs, rows, :] += pv

    def finish(p):
        for qs in range(2):
            o = []
            for a in range(2):
                rows = pl.ds(SPAN * a, SPAN)
                l = jnp.sum(l_v[qs, rows, :], axis=1, keepdims=True)
                o.append(acc_v[qs, rows, :] / l)
            both = jnp.where(lane < VDIM, o[0], o[1]).astype(BF16)
            os_v[p, 2 * qs] = both[:128]
            os_v[p, 2 * qs + 1] = both[128:]

    def o_z(p, d):
        to = lax.rem(z + d, MODEL)
        return remote(os_v.at[p, to], oall_v.at[dp, z, :, pl.ds(128 * p, 128)],
                      oz_ssem.at[p, d - 1], oz_rsem.at[p, d - 1], dev(m=to))

    def o_z_wait(p, d):
        src = lax.rem(z + MODEL - d, MODEL)
        remote(os_v.at[p, z], oall_v.at[dp, src, :, pl.ds(128 * p, 128)],
               oz_ssem.at[p, d - 1], oz_rsem.at[p, d - 1], dev()).wait_recv()

    def o_x(p, src_dp, to):
        part = oall_v.at[src_dp, :, :, pl.ds(128 * p, 128)]
        return remote(part, part, ox_ssem.at[p], ox_rsem.at[p], dev(d=to))

    def send_o(p):
        oall_v[dp, z, :, pl.ds(128 * p, 128)] = os_v[p, z]
        for d in (1, 2, 3):
            o_z(p, d).start()

    def pass_o(p):
        for d in (1, 2, 3):
            o_z_wait(p, d)
        o_x(p, dp, xn).start()

    for b in ORDER:
        scores(0, b)
    maxima(0)
    for p in range(PAIRS):
        for b in ORDER:
            if p + 1 < PAIRS:
                scores(p + 1, b)
            values(p, b)
        finish(p)
        if p + 1 < PAIRS:
            maxima(p + 1)
        send_o(p)
        if p >= 1:
            pass_o(p - 1)
        if p == 2:
            w_across(1)
            w_hop(2)
    w_across(2)
    w_hop(3)
    pass_o(PAIRS - 1)
    w_across(3)
    for j in (1, 2, 3):
        each_share(j, lambda s, sign: (wait_wd(s, 0), wait_wd(s, 1)))
    loads[9].wait()
    for p in range(PAIRS):
        o_x(p, xn, dp).wait_recv()

    def y_back():
        return remote(yst_v.at[0], out_h.at[:, pl.ds(pl.multiple_of(dp * NHALF, 128), NHALF)],
                      yb_ssem, yb_rsem, dev(d=xn))

    def y_local():
        return pltpu.make_async_copy(yst_v.at[1], out_h.at[:, pl.ds(pl.multiple_of(dp * NHALF, 128), NHALF)], yl_sem)

    for which in range(2):
        blk = xn if which == 0 else dp
        for n in range(NHALF // 256):
            cols = pl.ds(256 * n, 256)
            y = dot(oall_v[blk, 0], wall_v[0, :, cols])
            for s in range(1, MODEL):
                y = y + dot(oall_v[blk, s], wall_v[s, :, cols])
            yst_v[which, :, cols] = y.astype(BF16)
        if which == 0:
            y_back().start()
    y_local().start()

    kv_copy(ctx, 0, ynbr).wait_send()
    kv_copy(ctx, 1, partner).wait_send()
    kv_copy(ynbr, 2, partner).wait_send()

    @pl.when(z < MODEL - 1)
    def _():
        w_own(1).wait_send()

    @pl.when(z > 0)
    def _():
        w_own(0).wait_send()

    def sent(s, sign):
        to = z - sign

        @pl.when((to >= 0) & (to < MODEL))
        def _():
            w_fwd_z(s, to).wait_send()
        w_fwd_y(s).wait_send()
        w_fwd_d(s, 0).wait_send()
        w_fwd_d(s, 1).wait_send()

    for j in (1, 2, 3):
        each_share(j, sent)
    for p in range(PAIRS):
        for d in (1, 2, 3):
            o_z(p, d).wait_send()
        o_x(p, dp, xn).wait_send()
    y_back().wait_send()
    remote(yst_v.at[0], out_h.at[:, pl.ds(pl.multiple_of(xn * NHALF, 128), NHALF)], yb_ssem, yb_rsem, dev()).wait_recv()
    y_local().wait()


def layer(x, pos, freq, wdq, gq, wuq, wqr, wdkv, gkv, wkr, wuk, wuv, wout):
    vm = pl.BlockSpec(memory_space=pltpu.VMEM)
    hb = pl.BlockSpec(memory_space=pl.ANY)
    dma = pltpu.SemaphoreType.DMA
    return pl.pallas_call(
        kernel,
        out_shape=jax.ShapeDtypeStruct((ROWS // MODEL, HIDDEN), BF16),
        in_specs=[hb, vm, vm, vm, vm] + [hb] * 8,
        out_specs=hb,
        scratch_shapes=[
            pltpu.VMEM((ROWS, HIDDEN), BF16),
            pltpu.VMEM((HIDDEN, Q_RANK), BF16),
            pltpu.VMEM((Q_RANK, HEADS * NOPE), BF16),
            pltpu.VMEM((Q_RANK, HEADS * ROPE), BF16),
            pltpu.VMEM((HIDDEN, KV_RANK), BF16),
            pltpu.VMEM((HIDDEN, ROPE), BF16),
            pltpu.VMEM((HIDDEN, 128), BF16),
            pltpu.VMEM((KV_RANK, HEADS * NOPE), BF16),
            pltpu.VMEM((KV_RANK, HEADS * VDIM), BF16),
            pltpu.VMEM((ROWS, 128), F32),
            pltpu.VMEM((ROWS, 128), F32),
            pltpu.VMEM((KV_RANK, 1024), BF16),
            pltpu.VMEM((CTX, 2, SPAN + KRP, KV_RANK), BF16),
            pltpu.VMEM((ROWS, Q_RANK), BF16),
            pltpu.VMEM((PAIRS, 2, 2 * SPAN, 256), BF16),
            pltpu.VMEM((NSPAN, SPAN, HEADS * NOPE), BF16),
            pltpu.VMEM((NSPAN, SPAN, HEADS * VDIM), BF16),
            pltpu.VMEM((NSPAN, SPAN, 128), BF16),
            pltpu.VMEM((2, 9, 2 * SPAN, SPAN), F32),
            pltpu.VMEM((2, 2, 2 * SPAN, 128), F32),
            pltpu.VMEM((2, 2 * SPAN, 128), F32),
            pltpu.VMEM((2, 2 * SPAN, 128), F32),
            pltpu.VMEM((2, 2 * SPAN, 128), F32),
            pltpu.VMEM((PAIRS, MODEL, 128, 128), BF16),
            pltpu.VMEM((2, MODEL, 128, HV), BF16),
            pltpu.VMEM((MODEL, HV, NHALF), BF16),
            pltpu.VMEM((2, 128, NHALF), BF16),
            dma((10,)),
            dma((3,)), dma((3,)),
            dma((2,)), dma((MODEL,)), dma((MODEL,)),
            dma((MODEL,)), dma((MODEL,)),
            dma((MODEL, 2)), dma((MODEL, 2)),
            dma((PAIRS, 3)), dma((PAIRS, 3)),
            dma((PAIRS,)), dma((PAIRS,)),
            dma, dma, dma,
        ],
        compiler_params=pltpu.CompilerParams(collective_id=0, has_side_effects=True, vmem_limit_bytes=60 * 1024 * 1024),
        name='mla_layer',
    )(x, pos, freq, gq, gkv, wdq, wuq, wqr, wdkv, wkr, wuk, wuv, wout)


def solution(mesh):
    inv_freq = (ROPE_BASE ** (-(np.arange(ROPE // 2, dtype=np.float64) * 2.0 / ROPE))).astype(np.float32)
    freq = np.tile(inv_freq, 128 // (ROPE // 2))[None, :]

    def local(x_tokens, positions, w_dq, gain_q, w_uq, w_qr, w_dkv, gain_kv, w_kr, w_uk, w_uv, w_out):
        return layer(x_tokens, positions[None, :], jnp.asarray(freq), w_dq, gain_q[None, :], w_uq, w_qr, w_dkv,
                     gain_kv[None, :], w_kr, w_uk, w_uv, w_out)

    in_specs = (P(('dp', 'ctx'), None), P(('dp', 'ctx')), P(), P(), P(None, 'model'), P(None, 'model'), P(), P(), P(), P(None, 'model'), P(None, 'model'), P('model', None))
    out_specs = P(('dp', 'ctx', 'model'), None)
    return jax.shard_map(local, mesh=mesh, in_specs=in_specs, out_specs=out_specs, check_vma=False)
```

time: 245 us -> 78.6 us (0.32)
  waiting for transfers between devices: 107 us -> 0 us
  Pallas kernels: 0 us -> 70.7 us
  matrix products: 67.6 us -> 0 us
  local copies, waits for them, and re-layouts: 28.8 us -> 7.33 us
  other arithmetic: 18.8 us -> 0 us
  between operations: 13.6 us -> 0.01 us
  starting transfers between devices: 7.96 us -> 0 us
    reduce_scatter x1 -> x0, waiting for transfers between devices: 95.7 us -> none  [local(): lax.psum_scatter(y_part, 'model', scatter_dimension=0, tiled=True)]
    pallas_call x0 -> x1, Pallas kernels: none -> 70.7 us  [layer(): pl.pallas_call(kernel, out_shape=jax.ShapeDtypeStruct((ROWS // MODEL, HID...]
    dot_general x26 -> x0, matrix products: 67.6 us -> none  [the longest x4 12.2 us: merge_block(): jnp.einsum('qhr,kr->qhk', q_rope, kr_blk, preferred_element_type=jnp.floa...]
    convert_element_type x9 -> x0, local copies, waits for them, and re-layouts: 19.6 us -> none  [the longest x4 8.73 us: up_project(): jnp.dot(c_blk, w_uv, preferred_element_type=jnp.float32)]
    ppermute x6 -> x0, waiting for transfers between devices: 11.3 us -> none  [the longest x3 11.3 us: hop(): pos_blk = lax.ppermute(pos_blk, 'ctx', shift_perm)]
    ppermute x6 -> x0, starting transfers between devices: 7.96 us -> none  [the longest x3 7.44 us: hop(): pos_blk = lax.ppermute(pos_blk, 'ctx', shift_perm)]
    while x51 -> x0, local copies, waits for them, and re-layouts: 7.65 us -> none
    reduce_sum x4 -> x0, other arithmetic: 7.26 us -> none  [merge_block(): l_new = rescale * l_run + jnp.sum(exp_scores, axis=-1)]
  transfers between devices with their start and end apart: 7 -> 0, of which waited for: 4 -> 0; matrix products, arithmetic and copies ran while one was open for 0% -> 0% of each run, Pallas kernels for 0% -> 0%
where the time goes in v1:
time: 78.6 us; the launch traced here: 78 us
  Pallas kernels  70.7 us (90%)
  local copies, waits for them, and re-layouts  7.33 us (9%)
    pallas_call x1, Pallas kernels, layer(): pl.pallas_call(kernel, out_shape=jax.ShapeDtypeStruct((ROWS // MODEL, HID...  70.7 us
    unnamed x3, local copies, waits for them, and re-layouts  6.05 us

profile of v1, /device:TPU:0, one launch (start us, length us, event | category | flops | bytes accessed | tf_op | source)
XLA Modules:
  0.0 78.0 jit_solution(5685975964193418278)
XLA Ops:
  0.0 1.3 %broadcast_in_dim.10.gq_r = f32[1,768]{1,0:T(1,128)} reshape(f32[768]{0:T(1024)} %param.16) | data formatting | bytes 6144 | tf_op jit(solution)/shard_map/broadcast_in_dim | solution.py:469
  1.3 2.1 %copy.14.wqr_h = bf16[768,320]{1,0:T(8,128)(2,1)} copy(bf16[768,320]{0,1:T(8,128)(2,1)} %param.18) | data formatting | bytes 983040 | tf_op args[5]
  3.4 2.0 %copy.15.wkr_h = bf16[2560,32]{1,0:T(8,128)(2,1)} copy(bf16[2560,32]{0,1:T(8,128)(2,1)} %param.21) | data formatting | bytes 327680 | tf_op args[8]
  5.4 70.7 %mla_layer.1 = bf16[128,2560]{1,0:T(8,128)(2,1)} custom-call(bf16[512,2560]{1,0:T(8,128)(2,1)} %x_h.1, s32[1,512]{1,0:T(1,128)} %bitcast.2, f32[1,128]{1,0:T(1,128)} %constant.2.clone.freq_r, f32[1,768]{1,0:T(1,128)} %broadcast_in_dim.10.gq_r, f32[1,256]{1,0:T(1,128)} %bitcast.3, bf16[2560,768]{1,0:T(8,128)(2,1)} %wdq_h.1, bf16[768,640]{1,0:T(8,128)(2,1)} %wuq_h.1, ...), custom_call_target="tpu_custom_call" | custom-call | tf_op jit(solution)/shard_map/mla_layer/pallas_call | solution.py:417
  76.0 2.0 %copy.17 = bf16[128,2560]{1,0:T(8,128)(2,1)} copy(bf16[128,2560]{1,0:T(8,128)(2,1)} %mla_layer.1) | data formatting | bytes 1310720

commit v2 on v1

--- a/solution.py
+++ b/solution.py
@@ -28,6 +28,8 @@
 HV = HEADS * VDIM
 NHALF = HIDDEN // 2
 QROWS = HV // 4
+NSUB = 5
+SUBC = NHALF // NSUB
 KRP = SPAN // 8
 EPS = 1e-6
 ROPE_BASE = 10000.0
@@ -48,8 +50,8 @@
     return (h * lax.rsqrt(ms + EPS) * gain).astype(BF16)
 
 
-def kernel(x_h, pos_r, freq_r, gq_r, gkv_r, wdq_h, wuq_h, wqr_h, wdkv_h, wkr_h, wuk_h, wuv_h, wout_h, out_h,
-           x_v, wdq_v, wuq_v, wqr_v, wdkv_v, wkr_v, wkr4_v, wuk_v, wuv_v,
+def kernel(x_h, pos_h, freq_h, gq_h, gkv_h, wdq_h, wuq_h, wqr_h, wdkv_h, wkr_h, wuk_h, wuv_h, wout_h, out_h,
+           pos_r, freq_r, gq_r, gkv_r, x_v, wdq_v, wuq_v, wqr_v, wdkv_v, wkr_v, wuk_v, wuv_v,
            cos_v, sin_v, tile_v, lat_v, cq_v, qm_v, k_v, v_v, kr_v, s_v, mx_v, mb_v, l_v, acc_v,
            os_v, oall_v, wall_v, yst_v,
            lsem, kv_ssem, kv_rsem, wz_own, wz_ssem, wz_rsem, wy_ssem, wy_rsem, wd_ssem, wd_rsem,
@@ -72,6 +74,7 @@
     def local(src, dst, idx):
         return pltpu.make_async_copy(src, dst, lsem.at[idx])
 
+    small = [local(pos_h, pos_r, 10), local(freq_h, freq_r, 11), local(gq_h, gq_r, 12), local(gkv_h, gkv_r, 13)]
     loads = [
         local(wkr_h, wkr_v, 0),
         local(x_h.at[pl.ds(0, SPAN)], x_v.at[pl.ds(0, SPAN)], 1),
@@ -84,7 +87,7 @@
         local(wuv_h, wuv_v, 8),
         local(wout_h.at[:, pl.ds(pl.multiple_of(dp * NHALF, 128), NHALF)], wall_v.at[z], 9),
     ]
-    for c in loads:
+    for c in small + loads:
         c.start()
 
     barrier = pltpu.get_barrier_semaphore()
@@ -93,41 +96,47 @@
         pl.semaphore_signal(barrier, inc=1, device_id=p, device_id_type=MESH)
     pl.semaphore_wait(barrier, len(peers))
 
-    def wpiece(s, c):
-        return wall_v.at[s, pl.ds(pl.multiple_of(c * QROWS, 16), QROWS)]
-
-    wout_src = wout_h.at[pl.ds(pl.multiple_of(ctx * QROWS, 16), QROWS), pl.ds(pl.multiple_of(dp * NHALF, 128), NHALF)]
-
-    def w_own(up):
-        return remote(wout_src, wpiece(z, ctx), wz_own.at[up], wz_rsem.at[z], dev(m=z + 2 * up - 1))
-
-    def w_fwd_z(s, to):
-        return remote(wpiece(s, ctx), wpiece(s, ctx), wz_ssem.at[s], wz_rsem.at[s], dev(m=to))
-
-    def w_fwd_y(s):
-        return remote(wpiece(s, ctx), wpiece(s, ctx), wy_ssem.at[s], wy_rsem.at[s], dev(c=ynbr))
-
-    def w_fwd_d(s, which):
+    def wpiece(s, c, n=None):
+        rows = pl.ds(pl.multiple_of(c * QROWS, 16), QROWS)
+        return wall_v.at[s, rows] if n is None else wall_v.at[s, rows, pl.ds(SUBC * n, SUBC)]
+
+    def wsrc(n=None):
+        rows = pl.ds(pl.multiple_of(ctx * QROWS, 16), QROWS)
+        c0 = dp * NHALF + (0 if n is None else SUBC * n)
+        return wout_h.at[rows, pl.ds(pl.multiple_of(c0, 128), NHALF if n is None else SUBC)]
+
+    def w_own(up, n=None):
+        return remote(wsrc(n), wpiece(z, ctx, n), wz_own.at[up], wz_rsem.at[z, n or 0], dev(m=z + 2 * up - 1))
+
+    def w_fwd_z(s, to, n=None):
+        return remote(wpiece(s, ctx, n), wpiece(s, ctx, n), wz_ssem.at[s], wz_rsem.at[s, n or 0], dev(m=to))
+
+    def w_fwd_y(s, n=None):
+        return remote(wpiece(s, ctx, n), wpiece(s, ctx, n), wy_ssem.at[s], wy_rsem.at[s, n or 0], dev(c=ynbr))
+
+    def w_fwd_d(s, which, n=None):
         c = ctx if which == 0 else ynbr
-        return remote(wpiece(s, c), wpiece(s, c), wd_ssem.at[s, which], wd_rsem.at[s, which], dev(c=partner))
-
-    def wait_wz(s):
-        remote(wpiece(s, ctx), wpiece(s, ctx), wz_ssem.at[s], wz_rsem.at[s], dev()).wait_recv()
-
-    def wait_wy(s):
-        remote(wpiece(s, ynbr), wpiece(s, ynbr), wy_ssem.at[s], wy_rsem.at[s], dev()).wait_recv()
-
-    def wait_wd(s, which):
+        return remote(wpiece(s, c, n), wpiece(s, c, n), wd_ssem.at[s, which], wd_rsem.at[s, which, n or 0], dev(c=partner))
+
+    def wait_wz(s, n):
+        remote(wpiece(s, ctx, n), wpiece(s, ctx, n), wz_ssem.at[s], wz_rsem.at[s, n], dev()).wait_recv()
+
+    def wait_wy(s, n):
+        remote(wpiece(s, ynbr, n), wpiece(s, ynbr, n), wy_ssem.at[s], wy_rsem.at[s, n], dev()).wait_recv()
+
+    def wait_wd(s, which, n):
         c = partner if which == 0 else diag
-        remote(wpiece(s, c), wpiece(s, c), wd_ssem.at[s, which], wd_rsem.at[s, which], dev()).wait_recv()
+        remote(wpiece(s, c, n), wpiece(s, c, n), wd_ssem.at[s, which], wd_rsem.at[s, which, n], dev()).wait_recv()
 
     @pl.when(z < MODEL - 1)
     def _():
-        w_own(1).start()
+        for n in range(NSUB):
+            w_own(1, n).start()
 
     @pl.when(z > 0)
     def _():
-        w_own(0).start()
+        for n in range(NSUB):
+            w_own(0, n).start()
 
     def each_share(j, fn):
         for sign in (-1, 1):
@@ -137,25 +146,31 @@
             def _(s=s, sign=sign):
                 fn(s, sign)
 
-    def w_hop(j):
+    def hop(q):
+        j, n = q // NSUB + 1, q % NSUB
+
         def step(s, sign):
-            wait_wz(s)
+            wait_wz(s, n)
             to = z - sign
 
             @pl.when((to >= 0) & (to < MODEL))
             def _():
-                w_fwd_z(s, to).start()
-            w_fwd_y(s).start()
-            w_fwd_d(s, 0).start()
+                w_fwd_z(s, to, n).start()
+            w_fwd_y(s, n).start()
+            w_fwd_d(s, 0, n).start()
         each_share(j, step)
 
-    def w_across(j):
+    def across(q):
+        j, n = q // NSUB + 1, q % NSUB
+
         def step(s, sign):
-            wait_wy(s)
-            w_fwd_d(s, 1).start()
+            wait_wy(s, n)
+            w_fwd_d(s, 1, n).start()
         each_share(j, step)
 
     lane = lax.broadcasted_iota(jnp.int32, (1, 128), 1)
+    for c in small:
+        c.wait()
     for g in range(ROWS // 128):
         row = pos_r[:, pl.ds(128 * g, 128)].astype(F32)
         col = jnp.transpose(jnp.broadcast_to(row, (128, 128)), (1, 0))
@@ -173,11 +188,12 @@
         rot = jnp.where(low, -up, dn)
         return v * cos_v[pl.ds(r0, SPAN), :] + rot * sin_v[pl.ds(r0, SPAN), :]
 
+    def kv_copy(c, t, idx, to):
+        return remote(lat_v.at[c, t], lat_v.at[c, t], kv_ssem.at[idx, t], kv_rsem.at[idx, t], dev(c=to))
+
     loads[0].wait()
-    t_r = lax.broadcasted_iota(jnp.int32, (ROPE, 128), 0)
-    t_c = lax.broadcasted_iota(jnp.int32, (ROPE, 128), 1)
-    rep = jnp.where(t_r == t_c % ROPE, 1.0, 0.0).astype(BF16)
-    wkr4_v[...] = dot(wkr_v[...], rep).astype(BF16)
+    wkr4 = jnp.concatenate([wkr_v[...]] * 4, axis=0)
+    gkv = gkv_r[...]
     for t in range(2):
         r0 = t * SPAN
         if t == 0:
@@ -186,24 +202,27 @@
         else:
             loads[3].wait()
         xs = x_v[pl.ds(r0, SPAN), :]
-        lat_v[ctx, t, pl.ds(0, SPAN), :] = rms(dot(xs, wdkv_v[...]), gkv_r[...])
-        kr = rope(dot(xs, wkr4_v[...]), r0)
+        lat_v[ctx, t, pl.ds(0, SPAN), :] = rms(dot(xs, wdkv_v[...]), gkv)
+        kr = rope(dot_nt(xs, wkr4), r0)
         for half in range(2):
             packed = kr[128 * half:128 * half + KRP]
             for g in range(1, 4):
                 a = 128 * half + KRP * g
                 packed = jnp.where(lane // ROPE == g, kr[a:a + KRP], packed)
             lat_v[ctx, t, pl.ds(SPAN, KRP), pl.ds(128 * half, 128)] = packed.astype(BF16)
-
-    def kv_copy(c, idx, to):
-        return remote(lat_v.at[c], lat_v.at[c], kv_ssem.at[idx], kv_rsem.at[idx], dev(c=to))
-
-    kv_copy(ctx, 0, ynbr).start()
-    kv_copy(ctx, 1, partner).start()
+        if t == 0:
+            kv_copy(ctx, t, 0, ynbr).start()
+        else:
+            @pl.when(ctx >= 2)
+            def _():
+                kv_copy(ctx, 1, 0, ynbr).start()
+        kv_copy(ctx, t, 1, partner).start()
 
     loads[4].wait()
+    gq = jnp.concatenate([gq_r[g:g + 1, :] for g in range(Q_RANK // 128)], axis=1)
     for t in range(2):
-        cq_v[pl.ds(t * SPAN, SPAN), :] = rms(dot(x_v[pl.ds(t * SPAN, SPAN), :], wdq_v[...]), gq_r[...])
+        cq_v[pl.ds(t * SPAN, SPAN), :] = rms(dot(x_v[pl.ds(t * SPAN, SPAN), :], wdq_v[...]), gq)
+    hop(0)
     loads[5].wait()
     loads[6].wait()
     for t in range(2):
@@ -215,32 +234,56 @@
             qm_v[p, t, pl.ds(0, SPAN), pl.ds(0, 128)] = jnp.where(lane < NOPE, blk, zero)
             qm_v[p, t, pl.ds(SPAN, SPAN), pl.ds(0, 128)] = jnp.where(lane < NOPE, zero, blk)
         for b in range(3):
-            w = wqr_v[:, pl.ds(128 * b, 128)] if b < 2 else jnp.concatenate([wqr_v[:, pl.ds(256, 64)]] * 2, axis=1)
-            qr = rope(dot(cq, w), t * SPAN).astype(BF16)
+            w = wqr_v[pl.ds(128 * b, 128), :] if b < 2 else jnp.concatenate([wqr_v[pl.ds(256, 64), :]] * 2, axis=0)
+            qr = rope(dot_nt(cq, w), t * SPAN).astype(BF16)
             for h in range(4 * b, min(4 * b + 4, HEADS)):
                 qm_v[h // 2, t, pl.ds(SPAN * (h % 2), SPAN), pl.ds(128, 128)] = jnp.where(lane // ROPE == h % 4, qr, zero)
 
-    def up(c):
-        for t in range(2):
-            sp = c if t == 0 else NSPAN - 1 - c
-            lat = lat_v[c, t, pl.ds(0, SPAN), :]
-            k_v[sp] = dot(lat, wuk_v[...]).astype(BF16)
-            v_v[sp] = dot(lat, wuv_v[...]).astype(BF16)
-            big = dot(lat_v[c, t, pl.ds(SPAN, KRP), :], tile_v[...]).astype(BF16)
-            for g in range(8):
-                kr_v[sp, pl.ds(KRP * g, KRP), :] = big[:, 128 * g:128 * g + 128]
+    hop(1)
+
+    def up(c, t):
+        sp = c if t == 0 else NSPAN - 1 - c
+        lat = lat_v[c, t, pl.ds(0, SPAN), :]
+        k_v[sp] = dot(lat, wuk_v[...]).astype(BF16)
+        v_v[sp] = dot(lat, wuv_v[...]).astype(BF16)
+        big = dot(lat_v[c, t, pl.ds(SPAN, KRP), :], tile_v[...]).astype(BF16)
+        for g in range(8):
+            kr_v[sp, pl.ds(KRP * g, KRP), :] = big[:, 128 * g:128 * g + 128]
+
+    def up_late(c):
+        @pl.when(c >= ctx)
+        def _():
+            up(c, 1)
 
     loads[7].wait()
     loads[8].wait()
-    up(ctx)
-    kv_copy(partner, 1, ctx).wait_recv()
-    up(partner)
-    kv_copy(ynbr, 0, ctx).wait_recv()
-    kv_copy(ynbr, 2, partner).start()
-    up(ynbr)
-    w_hop(1)
-    kv_copy(diag, 2, ctx).wait_recv()
-    up(diag)
+    up(ctx, 0)
+    up(ctx, 1)
+    kv_copy(partner, 0, 1, ctx).wait_recv()
+    kv_copy(partner, 1, 1, ctx).wait_recv()
+    up(partner, 0)
+    up_late(partner)
+    hop(2)
+    kv_copy(ynbr, 0, 0, ctx).wait_recv()
+    kv_copy(ynbr, 0, 2, partner).start()
+    up(ynbr, 0)
+
+    @pl.when(ctx < 2)
+    def _():
+        kv_copy(ynbr, 1, 0, ctx).wait_recv()
+        kv_copy(ynbr, 1, 2, partner).start()
+        up(ynbr, 1)
+    hop(3)
+    across(0)
+    kv_copy(diag, 0, 2, ctx).wait_recv()
+    up(diag, 0)
+
+    @pl.when(ctx < 2)
+    def _():
+        kv_copy(diag, 1, 2, ctx).wait_recv()
+        up(diag, 1)
+    hop(4)
+    across(1)
 
     def block(b):
         if b < 5:
@@ -334,6 +377,15 @@
     for b in ORDER:
         scores(0, b)
     maxima(0)
+    hop(5)
+    across(2)
+    relay = {
+        0: lambda: (hop(6), across(3)),
+        1: lambda: (hop(7), across(4), hop(8)),
+        2: lambda: (across(5), hop(9), pass_o(0)),
+        3: lambda: (across(6), hop(10), pass_o(1), across(7)),
+        4: lambda: (hop(11), pass_o(2), across(8)),
+    }
     for p in range(PAIRS):
         for b in ORDER:
             if p + 1 < PAIRS:
@@ -343,51 +395,78 @@
         if p + 1 < PAIRS:
             maxima(p + 1)
         send_o(p)
-        if p >= 1:
-            pass_o(p - 1)
-        if p == 2:
-            w_across(1)
-            w_hop(2)
-    w_across(2)
-    w_hop(3)
-    pass_o(PAIRS - 1)
-    w_across(3)
-    for j in (1, 2, 3):
-        each_share(j, lambda s, sign: (wait_wd(s, 0), wait_wd(s, 1)))
+        relay[p]()
+    hop(12)
+    across(9)
+    pass_o(3)
+    hop(13)
+    across(10)
+    pass_o(4)
+    hop(14)
     loads[9].wait()
+
+    for t in range(2):
+        kv_copy(ctx, t, 1, partner).wait_send()
+    kv_copy(ctx, 0, 0, ynbr).wait_send()
+    kv_copy(ynbr, 0, 2, partner).wait_send()
+
+    @pl.when(ctx >= 2)
+    def _():
+        kv_copy(ctx, 1, 0, ynbr).wait_send()
+
+    @pl.when(ctx < 2)
+    def _():
+        kv_copy(ynbr, 1, 2, partner).wait_send()
+
+    @pl.when(z < MODEL - 1)
+    def _():
+        w_own(1).wait_send()
+
+    @pl.when(z > 0)
+    def _():
+        w_own(0).wait_send()
+
+    for p in range(PAIRS):
+        for d in (1, 2, 3):
+            o_z(p, d).wait_send()
+    across(11)
+    across(12)
     for p in range(PAIRS):
         o_x(p, xn, dp).wait_recv()
 
-    def y_back():
-        return remote(yst_v.at[0], out_h.at[:, pl.ds(pl.multiple_of(dp * NHALF, 128), NHALF)],
-                      yb_ssem, yb_rsem, dev(d=xn))
-
-    def y_local():
-        return pltpu.make_async_copy(yst_v.at[1], out_h.at[:, pl.ds(pl.multiple_of(dp * NHALF, 128), NHALF)], yl_sem)
-
-    for which in range(2):
-        blk = xn if which == 0 else dp
-        for n in range(NHALF // 256):
-            cols = pl.ds(256 * n, 256)
-            y = dot(oall_v[blk, 0], wall_v[0, :, cols])
-            for s in range(1, MODEL):
-                y = y + dot(oall_v[blk, s], wall_v[s, :, cols])
-            yst_v[which, :, cols] = y.astype(BF16)
-        if which == 0:
-            y_back().start()
-    y_local().start()
-
-    kv_copy(ctx, 0, ynbr).wait_send()
-    kv_copy(ctx, 1, partner).wait_send()
-    kv_copy(ynbr, 2, partner).wait_send()
-
-    @pl.when(z < MODEL - 1)
-    def _():
-        w_own(1).wait_send()
-
-    @pl.when(z > 0)
-    def _():
-        w_own(0).wait_send()
+    def ycols(half, n):
+        return out_h.at[:, pl.ds(pl.multiple_of(half * NHALF + SUBC * n, 128), SUBC)]
+
+    def y_back(n):
+        return remote(yst_v.at[xn, n], ycols(dp, n), yb_ssem.at[n], yb_rsem.at[n], dev(d=xn))
+
+    def y_come(n):
+        return remote(yst_v.at[xn, n], ycols(xn, n), yb_ssem.at[n], yb_rsem.at[n], dev())
+
+    def y_local(n):
+        return pltpu.make_async_copy(yst_v.at[dp, n], ycols(dp, n), yl_sem.at[n])
+
+    def final(n):
+        for j in (1, 2, 3):
+            each_share(j, lambda s, sign: (wait_wd(s, 0, n), wait_wd(s, 1, n)))
+        cols = pl.ds(SUBC * n, SUBC)
+        y = None
+        for s in range(MODEL):
+            o = jnp.concatenate([oall_v[0, s], oall_v[1, s]], axis=0)
+            part = dot(o, wall_v[s, :, cols])
+            y = part if y is None else y + part
+        yst_v[0, n] = y[:128].astype(BF16)
+        yst_v[1, n] = y[128:].astype(BF16)
+        y_back(n).start()
+        y_local(n).start()
+
+    final(0)
+    across(13)
+    final(1)
+    across(14)
+    final(2)
+    final(3)
+    final(4)
 
     def sent(s, sign):
         to = z - sign
@@ -402,31 +481,32 @@
     for j in (1, 2, 3):
         each_share(j, sent)
     for p in range(PAIRS):
-        for d in (1, 2, 3):
-            o_z(p, d).wait_send()
         o_x(p, dp, xn).wait_send()
-    y_back().wait_send()
-    remote(yst_v.at[0], out_h.at[:, pl.ds(pl.multiple_of(xn * NHALF, 128), NHALF)], yb_ssem, yb_rsem, dev()).wait_recv()
-    y_local().wait()
+    for n in range(NSUB):
+        y_back(n).wait_send()
+        y_local(n).wait()
+        y_come(n).wait_recv()
 
 
 def layer(x, pos, freq, wdq, gq, wuq, wqr, wdkv, gkv, wkr, wuk, wuv, wout):
-    vm = pl.BlockSpec(memory_space=pltpu.VMEM)
     hb = pl.BlockSpec(memory_space=pl.ANY)
     dma = pltpu.SemaphoreType.DMA
     return pl.pallas_call(
         kernel,
         out_shape=jax.ShapeDtypeStruct((ROWS // MODEL, HIDDEN), BF16),
-        in_specs=[hb, vm, vm, vm, vm] + [hb] * 8,
+        in_specs=[hb] * 13,
         out_specs=hb,
         scratch_shapes=[
+            pltpu.VMEM((1, ROWS), jnp.int32),
+            pltpu.VMEM((1, 128), F32),
+            pltpu.VMEM((Q_RANK // 128, 128), F32),
+            pltpu.VMEM((1, KV_RANK), F32),
             pltpu.VMEM((ROWS, HIDDEN), BF16),
             pltpu.VMEM((HIDDEN, Q_RANK), BF16),
             pltpu.VMEM((Q_RANK, HEADS * NOPE), BF16),
-            pltpu.VMEM((Q_RANK, HEADS * ROPE), BF16),
+            pltpu.VMEM((HEADS * ROPE, Q_RANK), BF16),
             pltpu.VMEM((HIDDEN, KV_RANK), BF16),
-            pltpu.VMEM((HIDDEN, ROPE), BF16),
-            pltpu.VMEM((HIDDEN, 128), BF16),
+            pltpu.VMEM((ROPE, HIDDEN), BF16),
             pltpu.VMEM((KV_RANK, HEADS * NOPE), BF16),
             pltpu.VMEM((KV_RANK, HEADS * VDIM), BF16),
             pltpu.VMEM((ROWS, 128), F32),
@@ -446,15 +526,15 @@
             pltpu.VMEM((PAIRS, MODEL, 128, 128), BF16),
             pltpu.VMEM((2, MODEL, 128, HV), BF16),
             pltpu.VMEM((MODEL, HV, NHALF), BF16),
-            pltpu.VMEM((2, 128, NHALF), BF16),
-            dma((10,)),
-            dma((3,)), dma((3,)),
-            dma((2,)), dma((MODEL,)), dma((MODEL,)),
-            dma((MODEL,)), dma((MODEL,)),
-            dma((MODEL, 2)), dma((MODEL, 2)),
+            pltpu.VMEM((2, NSUB, 128, SUBC), BF16),
+            dma((14,)),
+            dma((3, 2)), dma((3, 2)),
+            dma((2,)), dma((MODEL,)), dma((MODEL, NSUB)),
+            dma((MODEL,)), dma((MODEL, NSUB)),
+            dma((MODEL, 2)), dma((MODEL, 2, NSUB)),
             dma((PAIRS, 3)), dma((PAIRS, 3)),
             dma((PAIRS,)), dma((PAIRS,)),
-            dma, dma, dma,
+            dma((NSUB,)), dma((NSUB,)), dma((NSUB,)),
         ],
         compiler_params=pltpu.CompilerParams(collective_id=0, has_side_effects=True, vmem_limit_bytes=60 * 1024 * 1024),
         name='mla_layer',
@@ -466,8 +546,8 @@
     freq = np.tile(inv_freq, 128 // (ROPE // 2))[None, :]
 
     def local(x_tokens, positions, w_dq, gain_q, w_uq, w_qr, w_dkv, gain_kv, w_kr, w_uk, w_uv, w_out):
-        return layer(x_tokens, positions[None, :], jnp.asarray(freq), w_dq, gain_q[None, :], w_uq, w_qr, w_dkv,
-                     gain_kv[None, :], w_kr, w_uk, w_uv, w_out)
+        return layer(x_tokens, positions[None, :], jnp.asarray(freq), w_dq, gain_q.reshape(Q_RANK // 128, 128), w_uq,
+                     w_qr.T, w_dkv, gain_kv[None, :], w_kr.T, w_uk, w_uv, w_out)
 
     in_specs = (P(('dp', 'ctx'), None), P(('dp', 'ctx')), P(), P(), P(None, 'model'), P(None, 'model'), P(), P(), P(), P(None, 'model'), P(None, 'model'), P('model', None))
     out_specs = P(('dp', 'ctx', 'model'), None)

time: 78.6 us -> 65.8 us (0.84)
  Pallas kernels: 70.7 us -> 63.7 us
  local copies, waits for them, and re-layouts: 7.33 us -> 1.97 us
    pallas_call x1, Pallas kernels: 70.7 us -> 63.7 us  [layer(): pl.pallas_call(kernel, out_shape=jax.ShapeDtypeStruct((ROWS // MODEL, HID...]
    unnamed x3 -> x1, local copies, waits for them, and re-layouts: 6.05 us -> 1.97 us
    broadcast_in_dim x1 -> x0, local copies, waits for them, and re-layouts: 1.28 us -> none  [local(): gain_q[None, :]]
where the time goes in v2:
time: 65.8 us; the launch traced here: 65.7 us
  Pallas kernels  63.7 us (97%)
  local copies, waits for them, and re-layouts  1.97 us (3%)
    pallas_call x1, Pallas kernels, layer(): pl.pallas_call(kernel, out_shape=jax.ShapeDtypeStruct((ROWS // MODEL, HID...  63.7 us
    unnamed x1, local copies, waits for them, and re-layouts  1.97 us

profile of v2, /device:TPU:0, one launch (start us, length us, event | category | flops | bytes accessed | tf_op | source)
XLA Modules:
  0.0 65.7 jit_solution(3331150132676115935)
XLA Ops:
  0.0 63.7 %mla_layer.1 = bf16[128,2560]{1,0:T(8,128)(2,1)} custom-call(bf16[512,2560]{1,0:T(8,128)(2,1)} %x_h.1, s32[1,512]{1,0:T(1,128)} %bitcast.8, f32[1,128]{1,0:T(1,128)} %constant.2.clone.freq_h, f32[6,128]{1,0:T(8,128)} %bitcast.7, f32[1,256]{1,0:T(1,128)} %bitcast.9, bf16[2560,768]{1,0:T(8,128)(2,1)} %wdq_h.1, bf16[768,640]{1,0:T(8,128)(2,1)} %wuq_h.1, ...), custom_call_target="tpu_custom_call" | custom-call | tf_op jit(solution)/shard_map/mla_layer/pallas_call | solution.py:494
  63.7 2.0 %copy.15 = bf16[128,2560]{1,0:T(8,128)(2,1)} copy(bf16[128,2560]{1,0:T(8,128)(2,1)} %mla_layer.1) | data formatting | bytes 1310720

commit v3 on v2

--- a/solution.py
+++ b/solution.py
@@ -9,6 +9,17 @@
 from jax.sharding import PartitionSpec as P
 
 MESH = pl.DeviceIdType.MESH
+
+
+def scoped(fn):
+    @functools.wraps(fn)
+    def run(*args):
+        tag = "_".join(str(a) for a in args if isinstance(a, int))
+        with jax.named_scope(fn.__name__ + tag):
+            return fn(*args)
+    return run
+
+
 F32 = jnp.float32
 BF16 = jnp.bfloat16
 
@@ -51,9 +62,9 @@
 
 
 def kernel(x_h, pos_h, freq_h, gq_h, gkv_h, wdq_h, wuq_h, wqr_h, wdkv_h, wkr_h, wuk_h, wuv_h, wout_h, out_h,
-           pos_r, freq_r, gq_r, gkv_r, x_v, wdq_v, wuq_v, wqr_v, wdkv_v, wkr_v, wuk_v, wuv_v,
+           pos_r, freq_r, gq_r, gkv_r, x_v, wdq_v, wuq_v, wqr_v, wdkv_v, wkr_v, wkv_v,
            cos_v, sin_v, tile_v, lat_v, cq_v, qm_v, k_v, v_v, kr_v, s_v, mx_v, mb_v, l_v, acc_v,
-           os_v, oall_v, wall_v, yst_v,
+           os_v, oall_v, wall_v, yst_v, yacc_v,
            lsem, kv_ssem, kv_rsem, wz_own, wz_ssem, wz_rsem, wy_ssem, wy_rsem, wd_ssem, wd_rsem,
            oz_ssem, oz_rsem, ox_ssem, ox_rsem, yb_ssem, yb_rsem, yl_sem):
     dp = lax.axis_index('dp')
@@ -83,8 +94,8 @@
         local(wdq_h, wdq_v, 4),
         local(wuq_h, wuq_v, 5),
         local(wqr_h, wqr_v, 6),
-        local(wuk_h, wuk_v, 7),
-        local(wuv_h, wuv_v, 8),
+        local(wuk_h, wkv_v.at[:, pl.ds(0, HV)], 7),
+        local(wuv_h, wkv_v.at[:, pl.ds(HV, HV)], 8),
         local(wout_h.at[:, pl.ds(pl.multiple_of(dp * NHALF, 128), NHALF)], wall_v.at[z], 9),
     ]
     for c in small + loads:
@@ -94,7 +105,8 @@
     peers = [dev(m=lax.rem(z + d, MODEL)) for d in (1, 2, 3)] + [dev(d=xn), dev(c=partner), dev(c=ynbr)]
     for p in peers:
         pl.semaphore_signal(barrier, inc=1, device_id=p, device_id_type=MESH)
-    pl.semaphore_wait(barrier, len(peers))
+    with jax.named_scope('barrier'):
+        pl.semaphore_wait(barrier, len(peers))
 
     def wpiece(s, c, n=None):
         rows = pl.ds(pl.multiple_of(c * QROWS, 16), QROWS)
@@ -146,6 +158,7 @@
             def _(s=s, sign=sign):
                 fn(s, sign)
 
+    @scoped
     def hop(q):
         j, n = q // NSUB + 1, q % NSUB
 
@@ -160,6 +173,7 @@
             w_fwd_d(s, 0, n).start()
         each_share(j, step)
 
+    @scoped
     def across(q):
         j, n = q // NSUB + 1, q % NSUB
 
@@ -169,14 +183,16 @@
         each_share(j, step)
 
     lane = lax.broadcasted_iota(jnp.int32, (1, 128), 1)
-    for c in small:
-        c.wait()
-    for g in range(ROWS // 128):
-        row = pos_r[:, pl.ds(128 * g, 128)].astype(F32)
-        col = jnp.transpose(jnp.broadcast_to(row, (128, 128)), (1, 0))
-        ang = col * freq_r[...]
-        cos_v[pl.ds(128 * g, 128), :] = jnp.cos(ang)
-        sin_v[pl.ds(128 * g, 128), :] = jnp.sin(ang)
+    with jax.named_scope('small'):
+        for c in small:
+            c.wait()
+    with jax.named_scope('tables'):
+        for g in range(ROWS // 128):
+            row = pos_r[:, pl.ds(128 * g, 128)].astype(F32)
+            col = jnp.transpose(jnp.broadcast_to(row, (128, 128)), (1, 0))
+            ang = col * freq_r[...]
+            cos_v[pl.ds(128 * g, 128), :] = jnp.cos(ang)
+            sin_v[pl.ds(128 * g, 128), :] = jnp.sin(ang)
     rr = lax.broadcasted_iota(jnp.int32, (KV_RANK, 1024), 0)
     cc = lax.broadcasted_iota(jnp.int32, (KV_RANK, 1024), 1)
     tile_v[...] = jnp.where((rr // ROPE == cc // 128) & (rr % ROPE == cc % ROPE), 1.0, 0.0).astype(BF16)
@@ -194,58 +210,64 @@
     loads[0].wait()
     wkr4 = jnp.concatenate([wkr_v[...]] * 4, axis=0)
     gkv = gkv_r[...]
-    for t in range(2):
-        r0 = t * SPAN
-        if t == 0:
-            loads[1].wait()
-            loads[2].wait()
-        else:
-            loads[3].wait()
-        xs = x_v[pl.ds(r0, SPAN), :]
-        lat_v[ctx, t, pl.ds(0, SPAN), :] = rms(dot(xs, wdkv_v[...]), gkv)
-        kr = rope(dot_nt(xs, wkr4), r0)
-        for half in range(2):
-            packed = kr[128 * half:128 * half + KRP]
-            for g in range(1, 4):
-                a = 128 * half + KRP * g
-                packed = jnp.where(lane // ROPE == g, kr[a:a + KRP], packed)
-            lat_v[ctx, t, pl.ds(SPAN, KRP), pl.ds(128 * half, 128)] = packed.astype(BF16)
-        if t == 0:
-            kv_copy(ctx, t, 0, ynbr).start()
-        else:
-            @pl.when(ctx >= 2)
-            def _():
-                kv_copy(ctx, 1, 0, ynbr).start()
-        kv_copy(ctx, t, 1, partner).start()
-
-    loads[4].wait()
+    with jax.named_scope('ckv'):
+        for t in range(2):
+            r0 = t * SPAN
+            if t == 0:
+                loads[1].wait()
+                loads[2].wait()
+            else:
+                loads[3].wait()
+            xs = x_v[pl.ds(r0, SPAN), :]
+            lat_v[ctx, t, pl.ds(0, SPAN), :] = rms(dot(xs, wdkv_v[...]), gkv)
+            kr = rope(dot_nt(xs, wkr4), r0)
+            for half in range(2):
+                packed = kr[128 * half:128 * half + KRP]
+                for g in range(1, 4):
+                    a = 128 * half + KRP * g
+                    packed = jnp.where(lane // ROPE == g, kr[a:a + KRP], packed)
+                lat_v[ctx, t, pl.ds(SPAN, KRP), pl.ds(128 * half, 128)] = packed.astype(BF16)
+            if t == 0:
+                kv_copy(ctx, t, 0, ynbr).start()
+            else:
+                @pl.when(ctx >= 2)
+                def _():
+                    kv_copy(ctx, 1, 0, ynbr).start()
+            kv_copy(ctx, t, 1, partner).start()
+
+    with jax.named_scope('ld4'):
+        loads[4].wait()
     gq = jnp.concatenate([gq_r[g:g + 1, :] for g in range(Q_RANK // 128)], axis=1)
-    for t in range(2):
-        cq_v[pl.ds(t * SPAN, SPAN), :] = rms(dot(x_v[pl.ds(t * SPAN, SPAN), :], wdq_v[...]), gq)
+    with jax.named_scope('cq'):
+        for t in range(2):
+            cq_v[pl.ds(t * SPAN, SPAN), :] = rms(dot(x_v[pl.ds(t * SPAN, SPAN), :], wdq_v[...]), gq)
     hop(0)
     loads[5].wait()
     loads[6].wait()
-    for t in range(2):
-        cq = cq_v[pl.ds(t * SPAN, SPAN), :]
-        qn = dot(cq, wuq_v[...]).astype(BF16)
-        zero = jnp.zeros((SPAN, 128), BF16)
-        for p in range(PAIRS):
-            blk = qn[:, 128 * p:128 * p + 128]
-            qm_v[p, t, pl.ds(0, SPAN), pl.ds(0, 128)] = jnp.where(lane < NOPE, blk, zero)
-            qm_v[p, t, pl.ds(SPAN, SPAN), pl.ds(0, 128)] = jnp.where(lane < NOPE, zero, blk)
-        for b in range(3):
-            w = wqr_v[pl.ds(128 * b, 128), :] if b < 2 else jnp.concatenate([wqr_v[pl.ds(256, 64), :]] * 2, axis=0)
-            qr = rope(dot_nt(cq, w), t * SPAN).astype(BF16)
-            for h in range(4 * b, min(4 * b + 4, HEADS)):
-                qm_v[h // 2, t, pl.ds(SPAN * (h % 2), SPAN), pl.ds(128, 128)] = jnp.where(lane // ROPE == h % 4, qr, zero)
+    with jax.named_scope('qup'):
+        for t in range(2):
+            cq = cq_v[pl.ds(t * SPAN, SPAN), :]
+            qn = dot(cq, wuq_v[...]).astype(BF16)
+            zero = jnp.zeros((SPAN, 128), BF16)
+            for p in range(PAIRS):
+                blk = qn[:, 128 * p:128 * p + 128]
+                qm_v[p, t, pl.ds(0, SPAN), pl.ds(0, 128)] = jnp.where(lane < NOPE, blk, zero)
+                qm_v[p, t, pl.ds(SPAN, SPAN), pl.ds(0, 128)] = jnp.where(lane < NOPE, zero, blk)
+            for b in range(3):
+                w = wqr_v[pl.ds(128 * b, 128), :] if b < 2 else jnp.concatenate([wqr_v[pl.ds(256, 64), :]] * 2, axis=0)
+                qr = rope(dot_nt(cq, w), t * SPAN).astype(BF16)
+                for h in range(4 * b, min(4 * b + 4, HEADS)):
+                    qm_v[h // 2, t, pl.ds(SPAN * (h % 2), SPAN), pl.ds(128, 128)] = jnp.where(lane // ROPE == h % 4, qr, zero)
 
     hop(1)
 
+    @scoped
     def up(c, t):
         sp = c if t == 0 else NSPAN - 1 - c
         lat = lat_v[c, t, pl.ds(0, SPAN), :]
-        k_v[sp] = dot(lat, wuk_v[...]).astype(BF16)
-        v_v[sp] = dot(lat, wuv_v[...]).astype(BF16)
+        kv = dot(lat, wkv_v[...]).astype(BF16)
+        k_v[sp] = kv[:, :HV]
+        v_v[sp] = kv[:, HV:]
         big = dot(lat_v[c, t, pl.ds(SPAN, KRP), :], tile_v[...]).astype(BF16)
         for g in range(8):
             kr_v[sp, pl.ds(KRP * g, KRP), :] = big[:, 128 * g:128 * g + 128]
@@ -259,12 +281,14 @@
     loads[8].wait()
     up(ctx, 0)
     up(ctx, 1)
-    kv_copy(partner, 0, 1, ctx).wait_recv()
-    kv_copy(partner, 1, 1, ctx).wait_recv()
+    with jax.named_scope('kvw_partner'):
+        kv_copy(partner, 0, 1, ctx).wait_recv()
+        kv_copy(partner, 1, 1, ctx).wait_recv()
     up(partner, 0)
     up_late(partner)
     hop(2)
-    kv_copy(ynbr, 0, 0, ctx).wait_recv()
+    with jax.named_scope('kvw_ynbr'):
+        kv_copy(ynbr, 0, 0, ctx).wait_recv()
     kv_copy(ynbr, 0, 2, partner).start()
     up(ynbr, 0)
 
@@ -274,8 +298,8 @@
         kv_copy(ynbr, 1, 2, partner).start()
         up(ynbr, 1)
     hop(3)
-    across(0)
-    kv_copy(diag, 0, 2, ctx).wait_recv()
+    with jax.named_scope('kvw_diag'):
+        kv_copy(diag, 0, 2, ctx).wait_recv()
     up(diag, 0)
 
     @pl.when(ctx < 2)
@@ -283,7 +307,6 @@
         kv_copy(diag, 1, 2, ctx).wait_recv()
         up(diag, 1)
     hop(4)
-    across(1)
 
     def block(b):
         if b < 5:
@@ -313,6 +336,7 @@
                 m = jnp.maximum(mx_v[buf, qs, rows, :], m)
             mx_v[buf, qs, rows, :] = m
 
+    @scoped
     def maxima(p):
         buf = p % 2
         for qs in range(2):
@@ -339,6 +363,7 @@
                 l_v[qs, rows, :] += l
                 acc_v[qs, rows, :] += pv
 
+    @scoped
     def finish(p):
         for qs in range(2):
             o = []
@@ -350,90 +375,94 @@
             os_v[p, 2 * qs] = both[:128]
             os_v[p, 2 * qs + 1] = both[128:]
 
+    def oblk(blk, p, src):
+        return oall_v.at[pl.ds(pl.multiple_of(128 * blk, 128), 128), pl.ds(pl.multiple_of(512 * p + 128 * src, 128), 128)]
+
     def o_z(p, d):
         to = lax.rem(z + d, MODEL)
-        return remote(os_v.at[p, to], oall_v.at[dp, z, :, pl.ds(128 * p, 128)],
+        return remote(os_v.at[p, to], oblk(dp, p, z),
                       oz_ssem.at[p, d - 1], oz_rsem.at[p, d - 1], dev(m=to))
 
     def o_z_wait(p, d):
         src = lax.rem(z + MODEL - d, MODEL)
-        remote(os_v.at[p, z], oall_v.at[dp, src, :, pl.ds(128 * p, 128)],
+        remote(os_v.at[p, z], oblk(dp, p, src),
                oz_ssem.at[p, d - 1], oz_rsem.at[p, d - 1], dev()).wait_recv()
 
     def o_x(p, src_dp, to):
-        part = oall_v.at[src_dp, :, :, pl.ds(128 * p, 128)]
+        part = oall_v.at[pl.ds(pl.multiple_of(128 * src_dp, 128), 128), pl.ds(512 * p, 512)]
         return remote(part, part, ox_ssem.at[p], ox_rsem.at[p], dev(d=to))
 
+    @scoped
     def send_o(p):
-        oall_v[dp, z, :, pl.ds(128 * p, 128)] = os_v[p, z]
+        oblk(dp, p, z)[...] = os_v[p, z]
         for d in (1, 2, 3):
             o_z(p, d).start()
 
+    @scoped
     def pass_o(p):
         for d in (1, 2, 3):
             o_z_wait(p, d)
         o_x(p, dp, xn).start()
 
-    for b in ORDER:
-        scores(0, b)
+    with jax.named_scope('scores0'):
+        for b in ORDER:
+            scores(0, b)
     maxima(0)
     hop(5)
-    across(2)
     relay = {
-        0: lambda: (hop(6), across(3)),
-        1: lambda: (hop(7), across(4), hop(8)),
-        2: lambda: (across(5), hop(9), pass_o(0)),
-        3: lambda: (across(6), hop(10), pass_o(1), across(7)),
-        4: lambda: (hop(11), pass_o(2), across(8)),
+        0: lambda: (hop(6),),
+        1: lambda: (hop(7), hop(8)),
+        2: lambda: (hop(9), pass_o(0)),
+        3: lambda: (hop(10), pass_o(1)),
+        4: lambda: (hop(11), pass_o(2)),
     }
     for p in range(PAIRS):
-        for b in ORDER:
-            if p + 1 < PAIRS:
-                scores(p + 1, b)
-            values(p, b)
+        with jax.named_scope('attn%d' % p):
+            for b in ORDER:
+                if p + 1 < PAIRS:
+                    scores(p + 1, b)
+                values(p, b)
         finish(p)
         if p + 1 < PAIRS:
             maxima(p + 1)
         send_o(p)
         relay[p]()
+    for q in range(5):
+        across(q)
     hop(12)
-    across(9)
     pass_o(3)
+    for q in range(5, 10):
+        across(q)
     hop(13)
-    across(10)
     pass_o(4)
     hop(14)
     loads[9].wait()
 
-    for t in range(2):
-        kv_copy(ctx, t, 1, partner).wait_send()
-    kv_copy(ctx, 0, 0, ynbr).wait_send()
-    kv_copy(ynbr, 0, 2, partner).wait_send()
-
-    @pl.when(ctx >= 2)
-    def _():
-        kv_copy(ctx, 1, 0, ynbr).wait_send()
-
-    @pl.when(ctx < 2)
-    def _():
-        kv_copy(ynbr, 1, 2, partner).wait_send()
-
-    @pl.when(z < MODEL - 1)
-    def _():
-        w_own(1).wait_send()
-
-    @pl.when(z > 0)
-    def _():
-        w_own(0).wait_send()
-
-    for p in range(PAIRS):
-        for d in (1, 2, 3):
-            o_z(p, d).wait_send()
-    across(11)
-    across(12)
-    for p in range(PAIRS):
-        o_x(p, xn, dp).wait_recv()
-
+    with jax.named_scope('drain1'):
+        for t in range(2):
+            kv_copy(ctx, t, 1, partner).wait_send()
+        kv_copy(ctx, 0, 0, ynbr).wait_send()
+        kv_copy(ynbr, 0, 2, partner).wait_send()
+
+        @pl.when(ctx >= 2)
+        def _():
+            kv_copy(ctx, 1, 0, ynbr).wait_send()
+
+        @pl.when(ctx < 2)
+        def _():
+            kv_copy(ynbr, 1, 2, partner).wait_send()
+
+        @pl.when(z < MODEL - 1)
+        def _():
+            w_own(1).wait_send()
+
+        @pl.when(z > 0)
+        def _():
+            w_own(0).wait_send()
+
+        for p in range(PAIRS):
+            for d in (1, 2, 3):
+                o_z(p, d).wait_send()
     def ycols(half, n):
         return out_h.at[:, pl.ds(pl.multiple_of(half * NHALF + SUBC * n, 128), SUBC)]
 
@@ -446,27 +475,38 @@
     def y_local(n):
         return pltpu.make_async_copy(yst_v.at[dp, n], ycols(dp, n), yl_sem.at[n])
 
-    def final(n):
-        for j in (1, 2, 3):
-            each_share(j, lambda s, sign: (wait_wd(s, 0, n), wait_wd(s, 1, n)))
-        cols = pl.ds(SUBC * n, SUBC)
-        y = None
-        for s in range(MODEL):
-            o = jnp.concatenate([oall_v[0, s], oall_v[1, s]], axis=0)
-            part = dot(o, wall_v[s, :, cols])
-            y = part if y is None else y + part
+    def wcols(ps, n):
+        return jnp.concatenate([wall_v[s, pl.ds(128 * p, 128), pl.ds(SUBC * n, SUBC)] for p in ps for s in range(MODEL)], axis=0)
+
+    def have_w(n):
+        across(2 * NSUB + n)
+        with jax.named_scope('wdwait'):
+            for j in (1, 2, 3):
+                each_share(j, lambda s, sign: (wait_wd(s, 0, n), wait_wd(s, 1, n)))
+
+    def finish_y(n, y):
         yst_v[0, n] = y[:128].astype(BF16)
         yst_v[1, n] = y[128:].astype(BF16)
         y_back(n).start()
         y_local(n).start()
 
-    final(0)
-    across(13)
-    final(1)
-    across(14)
-    final(2)
-    final(3)
-    final(4)
+    EARLY = 2
+    with jax.named_scope('oxwait'):
+        for p in range(PAIRS - 1):
+            o_x(p, xn, dp).wait_recv()
+    for n in range(EARLY):
+        have_w(n)
+        with jax.named_scope('finala%d' % n):
+            yacc_v[n] = dot(oall_v[:, pl.ds(0, 2048)], wcols(range(PAIRS - 1), n))
+    with jax.named_scope('oxwait4'):
+        o_x(PAIRS - 1, xn, dp).wait_recv()
+    for n in range(EARLY):
+        with jax.named_scope('finalb%d' % n):
+            finish_y(n, yacc_v[n] + dot(oall_v[:, pl.ds(2048, 512)], wcols((PAIRS - 1,), n)))
+    for n in range(EARLY, NSUB):
+        have_w(n)
+        with jax.named_scope('final%d' % n):
+            finish_y(n, dot(oall_v[...], wcols(range(PAIRS), n)))
 
     def sent(s, sign):
         to = z - sign
@@ -478,14 +518,15 @@
         w_fwd_d(s, 0).wait_send()
         w_fwd_d(s, 1).wait_send()
 
-    for j in (1, 2, 3):
-        each_share(j, sent)
-    for p in range(PAIRS):
-        o_x(p, dp, xn).wait_send()
-    for n in range(NSUB):
-        y_back(n).wait_send()
-        y_local(n).wait()
-        y_come(n).wait_recv()
+    with jax.named_scope('drain2'):
+        for j in (1, 2, 3):
+            each_share(j, sent)
+        for p in range(PAIRS):
+            o_x(p, dp, xn).wait_send()
+        for n in range(NSUB):
+            y_back(n).wait_send()
+            y_local(n).wait()
+            y_come(n).wait_recv()
 
 
 def layer(x, pos, freq, wdq, gq, wuq, wqr, wdkv, gkv, wkr, wuk, wuv, wout):
@@ -507,8 +548,7 @@
             pltpu.VMEM((HEADS * ROPE, Q_RANK), BF16),
             pltpu.VMEM((HIDDEN, KV_RANK), BF16),
             pltpu.VMEM((ROPE, HIDDEN), BF16),
-            pltpu.VMEM((KV_RANK, HEADS * NOPE), BF16),
-            pltpu.VMEM((KV_RANK, HEADS * VDIM), BF16),
+            pltpu.VMEM((KV_RANK, 2 * HV), BF16),
             pltpu.VMEM((ROWS, 128), F32),
             pltpu.VMEM((ROWS, 128), F32),
             pltpu.VMEM((KV_RANK, 1024), BF16),
@@ -524,9 +564,10 @@
             pltpu.VMEM((2, 2 * SPAN, 128), F32),
             pltpu.VMEM((2, 2 * SPAN, 128), F32),
             pltpu.VMEM((PAIRS, MODEL, 128, 128), BF16),
-            pltpu.VMEM((2, MODEL, 128, HV), BF16),
+            pltpu.VMEM((2 * 128, HIDDEN), BF16),
             pltpu.VMEM((MODEL, HV, NHALF), BF16),
             pltpu.VMEM((2, NSUB, 128, SUBC), BF16),
+            pltpu.VMEM((2, 256, SUBC), F32),
             dma((14,)),
             dma((3, 2)), dma((3, 2)),
             dma((2,)), dma((MODEL,)), dma((MODEL, NSUB)),

time: 65.8 us -> 63.9 us (0.971)
  Pallas kernels: 63.7 us -> 61.8 us
    pallas_call x1, Pallas kernels: 63.7 us -> 61.8 us  [layer(): pl.pallas_call(kernel, out_shape=jax.ShapeDtypeStruct((ROWS // MODEL, HID...]
where the time goes in v3:
time: 63.9 us; the launch traced here: 63.8 us
  Pallas kernels  61.8 us (97%)
  local copies, waits for them, and re-layouts  1.97 us (3%)
    pallas_call x1, Pallas kernels, layer(): pl.pallas_call(kernel, out_shape=jax.ShapeDtypeStruct((ROWS // MODEL, HID...  61.8 us
    unnamed x1, local copies, waits for them, and re-layouts  1.97 us

profile of v3, /device:TPU:0, one launch (start us, length us, event | category | flops | bytes accessed | tf_op | source)
XLA Modules:
  0.0 63.8 jit_solution(1986819787148283354)
XLA Ops:
  0.0 61.8 %mla_layer.1 = bf16[128,2560]{1,0:T(8,128)(2,1)} custom-call(bf16[512,2560]{1,0:T(8,128)(2,1)} %x_h.1, s32[1,512]{1,0:T(1,128)} %bitcast.8, f32[1,128]{1,0:T(1,128)} %constant.2.clone.freq_h, f32[6,128]{1,0:T(8,128)} %bitcast.7, f32[1,256]{1,0:T(1,128)} %bitcast.9, bf16[2560,768]{1,0:T(8,128)(2,1)} %wdq_h.1, bf16[768,640]{1,0:T(8,128)(2,1)} %wuq_h.1, ...), custom_call_target="tpu_custom_call" | custom-call | tf_op jit(solution)/shard_map/mla_layer/pallas_call | solution.py:535
  61.8 2.0 %copy.15 = bf16[128,2560]{1,0:T(8,128)(2,1)} copy(bf16[128,2560]{1,0:T(8,128)(2,1)} %mla_layer.1) | data formatting | bytes 1310720
